TPU v7x, 128 devices: a whole 4x4x4 slice. The times are simulated.
128 devices in a mesh: replica: 1, data: 128 (over z, y, x, core).
Axes of the slice: x: 4, y: 4, z: 4, core: 2. Of those that a mesh axis runs over, the one named last changes fastest.
Arguments:
- q_hidden: bfloat16 [512, 32, 768], P(('replica', 'data'))
- d_hidden: bfloat16 [512, 180, 768], P(('replica', 'data'))
- w_proj: bfloat16 [768, 128], replicated
- q_mask: int32 [512, 32], P(('replica', 'data'))
- d_mask: int32 [512, 180], P(('replica', 'data'))
- temperature: float32 [], replicated
Outputs:
- output 1: float32 [512], P(('replica', 'data'))
- output 2: float32 [512], P(('replica', 'data'))
- output 3: float32 [1], P('replica')
All inputs are finite; a program needn't handle non-finite values.
Results may differ from a plain program's by a relative error of at most 0.001.
Values are sent between devices in bfloat16 or wider.
A program may use at most 1 GiB of HBM per device.

v0:
```python
import functools
import jax
import jax.numpy as jnp
from jax import lax
from jax.sharding import PartitionSpec as P

TILE_ELEMS = 8388608


def project(hidden, w_proj):
    raw_proj = jnp.einsum('bth,hk->btk', hidden, w_proj, preferred_element_type=jnp.float32)
    return (raw_proj / jnp.sqrt(jnp.sum(raw_proj * raw_proj, axis=-1, keepdims=True))).astype(jnp.bfloat16)


def blocks_per_step(total_blocks, block_elems):
    chosen = 1
    for candidate in range(1, total_blocks + 1):
        if total_blocks % candidate == 0 and candidate * block_elems <= TILE_ELEMS:
            chosen = candidate
    return chosen


def maxsim(q_vecs, p_vecs, d_mask):
    sim_vals = jnp.einsum('itk,jsk->itjs', q_vecs, p_vecs, preferred_element_type=jnp.float32)
    best_sim = jnp.max(jnp.where(d_mask[None, None, :, :] == 1, sim_vals, -jnp.inf), axis=3)
    return jnp.sum(best_sim, axis=1)


def solution(mesh):
    group_size = mesh.shape['data']
    batch_spec = P(('replica', 'data'))

    def local_loss(q_hidden, d_hidden, w_proj, q_mask, d_mask, value_a11):
        local_pairs = q_hidden.shape[0]
        q_len = q_hidden.shape[1]
        d_len = d_hidden.shape[1]
        proj_dim = w_proj.shape[1]
        q_vecs = jnp.where(q_mask[:, :, None] == 1, project(q_hidden, w_proj), 0.0).astype(jnp.bfloat16)
        p_vecs = project(d_hidden, w_proj)
        q_group = lax.all_gather(q_vecs, 'data', tiled=True)
        step_blocks = blocks_per_step(group_size, local_pairs * local_pairs * q_len * d_len)
        q_steps = q_group.reshape(group_size // step_blocks, step_blocks * local_pairs, q_len, proj_dim)
        col_scores = lax.map(functools.partial(maxsim, p_vecs=p_vecs, d_mask=d_mask), q_steps)
        col_scores = col_scores.reshape(group_size * local_pairs, local_pairs)
        row_scores = lax.all_to_all(col_scores, 'data', 0, 1, tiled=True)
        my_index = lax.axis_index('data')
        own_block = lax.dynamic_slice_in_dim(col_scores, my_index * local_pairs, local_pairs, axis=0)
        pos_logit = jnp.diagonal(own_block) / value_a11
        loss_query = jax.nn.logsumexp(row_scores / value_a11, axis=1) - pos_logit
        loss_doc = jax.nn.logsumexp(col_scores / value_a11, axis=0) - pos_logit
        group_sum = lax.psum(jnp.sum(loss_query + loss_doc), 'data')
        loss_mean = (group_sum / (2 * group_size * local_pairs)).reshape(1)
        return loss_query, loss_doc, loss_mean

    return jax.shard_map(local_loss, mesh=mesh, in_specs=(batch_spec, batch_spec, P(), batch_spec, batch_spec, P()), out_specs=(batch_spec, batch_spec, P('replica')), check_vma=False)
```

profile of v0, /device:TPU:1, one launch (start us, length us, event | category | flops | bytes accessed | tf_op | source)
XLA Modules:
  0.0 183.3 jit_solution(14157964084223906917)
XLA Ops:
  7.2 0.9 copy-done
  8.1 1.2 multiply_reduce_fusion.1
  9.3 0.7 broadcast_compare_fusion.1
  10.0 0.7 fusion.6
  10.7 1.8 multiply_reduce_fusion
  13.3 0.2 divide_convert_fusion
  13.4 68.0 %all-gather.2.cloned.1.call-done = bf16[512,32,128]{2,1,0:T(8,128)(2,1)} async-done(((bf16[4,32,128]{2,1,0:T(8,128)(2,1)}), bf16[512,32,128]{2,1,0:T(8,128)(2,1)}) %all-gather.2.cloned.1.call-update) | async-done | bytes 4194320 | tf_op jit(solution)/shard_map/all_gather | solution.py:40
  81.5 11.5 %while.10 = (s32[]{:T(128)}, f32[2,256,4]{1,2,0:T(4,128)S(1)}, s32[4,180]{1,0:T(4,128)S(1)}, bf16[2,256,32,128]{3,2,1,0:T(8,128)(2,1)}, bf16[4,180,128]{2,1,0:T(8,128)(2,1)S(1)}, /*index=5*/s32[]{:T(128)}, f32[]{:T(128)}) while((s32[]{:T(128)}, f32[2,256,4]{1,2,0:T(4,128)S(1)}, s32[4,180]{1,0:T(4,128)S(1)}, ...), condition=%wide.region_5.6_spmd, body=%wide.region_2.5_spmd.sunk | while | flops 1521745664 | bytes 6754617 | solution.py:43
  81.5 2.0 %constant_dynamic-slice_fusion.3 = bf16[1,256,32,128]{3,2,1,0:T(8,128)(2,1)S(1)} fusion(bf16[2,256,32,128]{3,2,1,0:T(8,128)(2,1)} %get-tuple-element.115, s32[]{:T(128)} %get-tuple-element.105), kind=kLoop, calls=%fused_computation.6.clone.1 | loop fusion | bytes 4194308 | tf_op jit(solution)/shard_map/while/body/jit(dynamic_index_in_dim)/dynamic_slice | solution.py:43
  83.4 3.7 %select_reduce_fusion.2 = f32[256,32,4]{0,2,1:T(4,128)S(1)} fusion(pred[4,180]{1,0:T(4,128)(4,1)S(1)} %broadcast_compare_fusion.3, bf16[1,256,32,128]{3,2,1,0:T(8,128)(2,1)S(1)} %constant_dynamic-slice_fusion.3, bf16[4,180,128]{2,1,0:T(8,128)(2,1)S(1)} %get-tuple-element.116), kind=kOutput, calls=%fused_computation.1.clone.1 | convolution fusion | flops 1521713152 | bytes 2413264 | tf_op jit(solution)/shard_map/while/body/eval_jaxpr/itk,jsk->itjs/dot_general | solution.py:24
  87.2 2.0 %constant_dynamic-slice_fusion.3 = bf16[1,256,32,128]{3,2,1,0:T(8,128)(2,1)S(1)} fusion(bf16[2,256,32,128]{3,2,1,0:T(8,128)(2,1)} %get-tuple-element.115, s32[]{:T(128)} %get-tuple-element.105), kind=kLoop, calls=%fused_computation.6.clone.1 | loop fusion | bytes 4194308 | tf_op jit(solution)/shard_map/while/body/jit(dynamic_index_in_dim)/dynamic_slice | solution.py:43
  89.2 3.7 %select_reduce_fusion.2 = f32[256,32,4]{0,2,1:T(4,128)S(1)} fusion(pred[4,180]{1,0:T(4,128)(4,1)S(1)} %broadcast_compare_fusion.3, bf16[1,256,32,128]{3,2,1,0:T(8,128)(2,1)S(1)} %constant_dynamic-slice_fusion.3, bf16[4,180,128]{2,1,0:T(8,128)(2,1)S(1)} %get-tuple-element.116), kind=kOutput, calls=%fused_computation.1.clone.1 | convolution fusion | flops 1521713152 | bytes 2413264 | tf_op jit(solution)/shard_map/while/body/eval_jaxpr/itk,jsk->itjs/dot_general | solution.py:24
  93.0 0.3 all_to_all.10
  93.3 0.9 copy.18
  94.2 5.3 %all-to-all-start = ((f32[128,4,4]{1,2,0:T(4,128)}), f32[128,4,4]{1,2,0:T(4,128)S(1)}, u32[]{:S(2)}, u32[]{:S(2)}) async-start(f32[128,4,4]{1,2,0:T(4,128)} %copy.18), calls=%async_computation | async-start | bytes 524288 | tf_op jit(solution)/shard_map/all_to_all | solution.py:45
  99.5 0.1 fusion.7
  99.6 0.2 exponential_reduce_fusion.1
  99.9 0.1 copy.22
  100.0 0.6 gather_fusion
  100.6 9.7 %all-to-all-done = f32[128,4,4]{1,2,0:T(4,128)S(1)} async-done(((f32[128,4,4]{1,2,0:T(4,128)}), f32[128,4,4]{1,2,0:T(4,128)S(1)}, u32[]{:S(2)}, u32[]{:S(2)}) %all-to-all-start) | async-done | bytes 8224 | tf_op jit(solution)/shard_map/all_to_all | solution.py:45
  110.3 0.2 fusion.8
  110.5 0.2 exponential_reduce_fusion
  110.7 1.1 add_reduce_fusion
  111.8 62.8 %psum.7 = f32[]{:T(128)} all-reduce(f32[]{:T(128)} %get-tuple-element.56), channel_id=1, replica_groups=mesh['replica'=1,'data'=128] {'data'}, use_global_device_ids=true, to_apply=%region_11.12 | all-reduce | flops 1 | bytes 8 | tf_op jit(solution)/shard_map/psum | solution.py:51
  (19 shorter events, 0.3 us)
Async XLA Ops:
  7.2 0.9 copy-start
  7.2 74.3 %copy-start.1 = (s32[4,180]{1,0:T(4,128)S(1)}, s32[4,180]{1,0:T(4,128)}, u32[]{:S(2)}) copy-start(s32[4,180]{1,0:T(4,128)} %param.12) | copy-start | bytes 8644
  7.2 74.3 %all-gather.2.cloned.1.call-start = ((), (), s32[]{:S(2)}) async-start(), calls=%async_computation.1 | async-start | bytes 4227072 | tf_op jit(solution)/shard_map/all_gather | solution.py:40
  94.2 16.2 %all-to-all-start = ((f32[128,4,4]{1,2,0:T(4,128)}), f32[128,4,4]{1,2,0:T(4,128)S(1)}, u32[]{:S(2)}, u32[]{:S(2)}) async-start(f32[128,4,4]{1,2,0:T(4,128)} %copy.18), calls=%async_computation | async-start | bytes 524288 | tf_op jit(solution)/shard_map/all_to_all | solution.py:45
Sparse Core Ops, SparseCore 0:
  11.1 70.2 all-gather.1
where the time goes:
time: 184 us; the launch traced here: 183 us
  waiting for transfers between devices  77.8 us (42%)
  blocking collectives  62.8 us (34%)
  between operations  16.6 us (9%)
  matrix products  10.5 us (6%)
  local copies, waits for them, and re-layouts  6.77 us (4%)
  starting transfers between devices  5.34 us (3%)
  other arithmetic  3.45 us (2%)
    all_gather x1, waiting for transfers between devices, local_loss(): q_group = lax.all_gather(q_vecs, 'data', tiled=True)  68 us
    psum x1, blocking collectives, local_loss(): group_sum = lax.psum(jnp.sum(loss_query + loss_doc), 'data')  62.8 us
    all_to_all x1, waiting for transfers between devices, local_loss(): row_scores = lax.all_to_all(col_scores, 'data', 0, 1, tiled=True)  9.72 us
    dot_general x2, matrix products, maxsim(): jnp.einsum('itk,jsk->itjs', q_vecs, p_vecs, preferred_element_type=jnp.fl...  7.47 us
    all_to_all x1, starting transfers between devices, local_loss(): row_scores = lax.all_to_all(col_scores, 'data', 0, 1, tiled=True)  5.31 us
    dynamic_slice x2, local copies, waits for them, and re-layouts, local_loss(): lax.map(functools.partial(maxsim, p_vecs=p_vecs, d_mask=d_mask), q_steps)  3.91 us
  transfers between devices with their start and end apart: 2, of which 2 were waited for; matrix products, arithmetic and copies ran while one was open for 2% of the time, Pallas kernels for 0%

commit v1 on v0

v1 whole, which is shorter than its diff:
```python
import functools
import jax
import jax.numpy as jnp
from jax import lax
from jax.experimental import pallas as pl
from jax.experimental.pallas import tpu as pltpu
from jax.sharding import PartitionSpec as P

F32 = jnp.float32
BF16 = jnp.bfloat16
MESH = pl.DeviceIdType.MESH
NZ, NY, NX, NC = 4, 4, 4, 2
DPAD = 184


def unit_rows(raw):
    return raw / jnp.sqrt(jnp.sum(raw * raw, axis=-1, keepdims=True))


def kernel(q_hbm, d_hbm, w_hbm, qm_hbm, dm_hbm, temp_ref, lq_ref, ld_ref, lm_ref,
           qh, dh, w, qm, dm, qbuf, dbuf, best, rowbuf, colbuf, row2, col2,
           lsem, qs, qr, ds_, dr, ps, pr, rs, rr, cs, cr, rs2, rr2, cs2, cr2):
    me = lax.axis_index('data')
    c = lax.rem(me, 2)
    x = lax.rem(me // 2, 4)
    y = lax.rem(me // 8, 4)
    z = me // 32

    def dev(z_, y_, x_, c_):
        return {'data': ((z_ * 4 + y_) * 4 + x_) * 2 + c_}

    def plane(r):
        return lax.rem(z + r // 4, 4), lax.rem(y + r % 4, 4)

    def plane_back(r):
        return lax.rem(z + 4 - r // 4, 4), lax.rem(y + 4 - r % 4, 4)

    def line(r):
        return lax.rem(x + r // 2, 4), lax.rem(c + r % 2, 2)

    def line_back(r):
        return lax.rem(x + 4 - r // 2, 4), lax.rem(c + r % 2, 2)

    loads = [pltpu.make_async_copy(w_hbm, w, lsem.at[0]),
             pltpu.make_async_copy(q_hbm, qh, lsem.at[1]),
             pltpu.make_async_copy(qm_hbm, qm, lsem.at[2]),
             pltpu.make_async_copy(dm_hbm, dm, lsem.at[3])]
    loads += [pltpu.make_async_copy(d_hbm.at[j], dh.at[j], lsem.at[4 + j]) for j in range(4)]
    for cp in loads:
        cp.start()

    barrier = pltpu.get_barrier_semaphore()
    for r in range(1, 16):
        zz, yy = plane(r)
        pl.semaphore_signal(barrier, inc=1, device_id=dev(zz, yy, x, c), device_id_type=MESH)
    for r in range(1, 8):
        xx, cc = line(r)
        pl.semaphore_signal(barrier, inc=1, device_id=dev(z, y, xx, cc), device_id_type=MESH)

    for cp in loads[:4]:
        cp.wait()
    q_raw = jnp.dot(qh[...].reshape(128, 768), w[...], preferred_element_type=F32)
    q_col = jnp.transpose(jnp.concatenate([qm[...].astype(F32), jnp.zeros((4, 32), F32)], axis=0))
    q_valid = jnp.concatenate([q_col[:, i:i + 1] for i in range(4)], axis=0)
    q_unit = jnp.where(q_valid == 1.0, unit_rows(q_raw), 0.0).astype(BF16)
    my_slot = z * 4 + y
    qbuf[my_slot] = q_unit

    pl.semaphore_wait(barrier, 22)

    def q_copy(r):
        zz, yy = plane_back(r)
        return pltpu.make_async_remote_copy(qbuf.at[my_slot], qbuf.at[my_slot], qs.at[r], qr.at[r],
                                            device_id=dev(zz, yy, x, c), device_id_type=MESH)

    q_order = [1, 3, 4, 12, 5, 15, 7, 13, 2, 8, 6, 9, 14, 11, 10]
    for r in q_order:
        q_copy(r).start()

    d_col = jnp.transpose(jnp.concatenate([dm[...].astype(F32), jnp.zeros((4, 180), F32)], axis=0))
    pos = lax.broadcasted_iota(jnp.int32, (180, 1), 0)

    def piece(xx, cc, h):
        return dbuf.at[xx, cc, h]

    def d_copy(xx, cc, h, to, ssem, rsem):
        return pltpu.make_async_remote_copy(piece(xx, cc, h), piece(xx, cc, h), ssem, rsem,
                                            device_id=to, device_id_type=MESH)

    xr, xl, xo, cp_ = lax.rem(x + 1, 4), lax.rem(x + 3, 4), lax.rem(x + 2, 4), 1 - c
    right, left, partner = dev(z, y, xr, c), dev(z, y, xl, c), dev(z, y, x, cp_)
    sends = []

    def send(cp):
        cp.start()
        sends.append(cp)

    for h in range(2):
        parts = []
        for j in (2 * h, 2 * h + 1):
            loads[4 + j].wait()
            u = unit_rows(jnp.dot(dh[j], w[...], preferred_element_type=F32))
            valid = d_col[:, j:j + 1] == 1.0
            first = jnp.min(jnp.where(valid, pos, 1000), axis=0, keepdims=True)
            vec = jnp.sum(jnp.where(pos == first, u, 0.0), axis=0, keepdims=True)
            u = jnp.where(valid, u, vec)
            parts += [u, jnp.broadcast_to(vec, (DPAD - 180, 128))]
        dbuf[x, c, h] = jnp.concatenate(parts, axis=0).astype(BF16)
        send(d_copy(x, c, h, right, ds_.at[h], dr.at[h]))
        send(d_copy(x, c, h, left, ds_.at[2 + h], dr.at[2 + h]))
        send(d_copy(x, c, h, partner, ps.at[h], pr.at[h]))

    def wait_ici(i):
        xx, h = [(xl, 0), (xl, 1), (xr, 0), (xr, 1), (xo, 0), (xo, 1)][i]
        d_copy(xx, c, h, right, ds_.at[i], dr.at[i]).wait_recv()
        if i == 0:
            send(d_copy(xl, c, 0, right, ds_.at[4], dr.at[4]))
        if i == 3:
            send(d_copy(xr, c, 1, left, ds_.at[5], dr.at[5]))
        send(d_copy(xx, c, h, partner, ps.at[2 + i], pr.at[2 + i]))

    def wait_partner(i):
        xx, h = [(x, 0), (x, 1), (xl, 0), (xl, 1), (xr, 0), (xr, 1), (xo, 0), (xo, 1)][i]
        d_copy(xx, cp_, h, partner, ps.at[i], pr.at[i]).wait_recv()

    def wait_q(r):
        q_copy(r).wait_recv()

    def unit(xx, k):
        r = 2 * k
        slots = []
        for rr_ in (r, r + 1):
            zz, yy = lax.rem(z + rr_ // 4, 4), lax.rem(y + lax.rem(rr_, 4), 4)
            slots.append(zz * 4 + yy)
        rhs = jnp.concatenate([qbuf[s] for s in slots], axis=0)
        lhs = dbuf[xx].reshape(8 * DPAD, 128)
        sim = lax.dot_general(lhs, rhs, (((1,), (1,)), ((), ())), preferred_element_type=F32)
        top = jnp.max(sim.reshape(8, DPAD, 256), axis=1)
        row = pl.ds(pl.multiple_of(xx * 8, 8), 8)
        for i in range(2):
            best[row, pl.ds(pl.multiple_of(slots[i] * 128, 128), 128)] = top[:, i * 128:(i + 1) * 128]

    wait_partner(0)
    wait_partner(1)

    def q_loop(lo, hi):
        def body(k, carry):
            @pl.when(k > 0)
            def _():
                q_copy_dyn(2 * k).wait_recv()
            q_copy_dyn(2 * k + 1).wait_recv()
            unit(x, k)
            return carry
        lax.fori_loop(lo, hi, body, 0)

    def q_copy_dyn(r):
        zz, yy = lax.rem(z + 4 - r // 4, 4), lax.rem(y + 4 - lax.rem(r, 4), 4)
        return pltpu.make_async_remote_copy(qbuf.at[my_slot], qbuf.at[my_slot], qs.at[r], qr.at[r],
                                            device_id=dev(zz, yy, x, c), device_id_type=MESH)

    q_loop(0, 2)
    wait_ici(0)
    wait_ici(2)
    q_loop(2, 4)
    wait_ici(1)
    wait_ici(3)
    q_loop(4, 8)

    def d_loop(xx):
        def body(k, carry):
            unit(xx, k)
            return carry
        lax.fori_loop(0, 8, body, 0)

    wait_partner(2)
    wait_partner(3)
    d_loop(xl)
    wait_ici(4)
    wait_ici(5)
    wait_partner(4)
    wait_partner(5)
    d_loop(xr)
    wait_partner(6)
    wait_partner(7)
    d_loop(xo)

    b = best[...]
    hi = b.astype(BF16)
    rest = b - hi.astype(F32)
    mid = rest.astype(BF16)
    low = (rest - mid.astype(F32)).astype(BF16)
    tok = lax.broadcasted_iota(jnp.int32, (2048, 128), 0) // 32
    pick = (tok == lax.broadcasted_iota(jnp.int32, (2048, 128), 1)).astype(F32).astype(BF16)
    sums = jnp.dot(jnp.concatenate([hi, mid, low], axis=0), pick, preferred_element_type=F32)
    logits = ((sums[0:32] + sums[32:64]) + sums[64:96]) / temp_ref[0]
    lane = lax.broadcasted_iota(jnp.int32, (32, 128), 1)
    sub = lax.broadcasted_iota(jnp.int32, (32, 128), 0)
    lane1 = lax.broadcasted_iota(jnp.int32, (1, 128), 1)
    own_row = (sub // 4) == (x * 2 + c)
    own = own_row & (lane - my_slot * 4 == lax.rem(sub, 4))
    pos_q = jnp.sum(jnp.where(own, logits, 0.0), axis=0, keepdims=True)
    pos_total = jnp.sum(pos_q, axis=1, keepdims=True)
    m_row = jnp.max(logits, axis=0, keepdims=True)
    l_row = jnp.sum(jnp.exp(logits - m_row), axis=0, keepdims=True)
    qlane = lane < 64
    m_col = jnp.max(jnp.where(qlane, logits, -jnp.inf), axis=1, keepdims=True)
    l_col = jnp.sum(jnp.where(qlane, jnp.exp(logits - m_col), 0.0), axis=1, keepdims=True)
    m_colr = jnp.sum(jnp.where(sub == lane, m_col, 0.0), axis=0, keepdims=True)
    l_colr = jnp.sum(jnp.where(sub == lane - 32, l_col, 0.0), axis=0, keepdims=True)
    rowbuf[my_slot] = jnp.where(lane1 < 64, m_row, pltpu.roll(l_row, 64, 1))
    my_line = x * 2 + c
    colbuf[my_line] = jnp.where(lane1 == 64, pos_total, m_colr + l_colr)

    def plane_copy(buf, r, ss, rs_):
        zz, yy = plane_back(r)
        return pltpu.make_async_remote_copy(buf.at[my_slot], buf.at[my_slot], ss.at[r], rs_.at[r],
                                            device_id=dev(zz, yy, x, c), device_id_type=MESH)

    def line_copy(buf, r, ss, rs_):
        xx, cc = line_back(r)
        return pltpu.make_async_remote_copy(buf.at[my_line], buf.at[my_line], ss.at[r], rs_.at[r],
                                            device_id=dev(z, y, xx, cc), device_id_type=MESH)

    far_first = [10, 9, 11, 6, 14, 2, 8, 5, 7, 13, 15, 1, 3, 4, 12]
    rows1 = [plane_copy(rowbuf, r, rs, rr) for r in far_first]
    cols1 = [line_copy(colbuf, r, cs, cr) for r in (5, 4, 3, 7, 2, 6, 1)]
    for cp in rows1 + cols1:
        cp.start()
    for cp in cols1 + rows1:
        cp.wait_recv()
    rb = rowbuf[...].reshape(16, 128)
    rb_l = pltpu.roll(rb, 64, 1)
    m = jnp.max(rb, axis=0, keepdims=True)
    lse_row = m + jnp.log(jnp.sum(rb_l * jnp.exp(rb - m), axis=0, keepdims=True))
    row_total = jnp.sum(jnp.where(lane1 < 64, lse_row, 0.0), axis=1, keepdims=True)
    cb = colbuf[...].reshape(8, 128)
    cb_l = pltpu.roll(cb, 96, 1)
    mc = jnp.max(cb, axis=0, keepdims=True)
    lse_col = mc + jnp.log(jnp.sum(cb_l * jnp.exp(cb - mc), axis=0, keepdims=True))
    col_total = jnp.sum(jnp.where(lane1 < 32, lse_col, 0.0), axis=1, keepdims=True)
    pos_sum = jnp.sum(jnp.sum(jnp.where(lane1 == 64, cb, 0.0), axis=0, keepdims=True), axis=1, keepdims=True)
    row2[my_slot] = jnp.broadcast_to(col_total - 2.0 * pos_sum, (1, 128))
    col2[my_line] = jnp.broadcast_to(row_total, (1, 128))
    rows2 = [plane_copy(row2, r, rs2, rr2) for r in far_first]
    cols2 = [line_copy(col2, r, cs2, cr2) for r in (5, 4, 3, 7, 2, 6, 1)]
    for cp in rows2 + cols2:
        cp.start()
    src = lax.broadcasted_iota(jnp.int32, (128, 128), 0)
    dst = lax.broadcasted_iota(jnp.int32, (128, 128), 1)

    def to_front(v, start):
        return pltpu.roll(v, lax.rem(128 - start, 128), 1)

    pos_front = to_front(pos_q, my_slot * 4)
    lq_ref[...] = to_front(lse_row, my_slot * 4) - pos_front
    ld_ref[...] = to_front(lse_col, my_line * 4) - pos_front
    for cp in cols2 + rows2:
        cp.wait_recv()
    total = (jnp.sum(row2[...].reshape(16, 128), axis=0, keepdims=True)
             + jnp.sum(col2[...].reshape(8, 128), axis=0, keepdims=True))
    lm_ref[...] = total / 1024.0

    for r in q_order:
        q_copy(r).wait_send()
    for cp in sends + rows1 + cols1 + rows2 + cols2:
        cp.wait_send()


def solution(mesh):
    batch_spec = P(('replica', 'data'))

    def local_loss(q_hidden, d_hidden, w_proj, q_mask, d_mask, temperature):
        any_spec = pl.BlockSpec(memory_space=pl.ANY)
        vmem = pl.BlockSpec(memory_space=pltpu.VMEM)
        dma = pltpu.SemaphoreType.DMA
        out = jax.ShapeDtypeStruct((1, 128), F32)
        lq, ld, lm = pl.pallas_call(
            kernel,
            out_shape=(out, out, out),
            in_specs=[any_spec] * 5 + [pl.BlockSpec(memory_space=pltpu.SMEM)],
            out_specs=(vmem, vmem, vmem),
            scratch_shapes=[
                pltpu.VMEM((4, 32, 768), BF16),
                pltpu.VMEM((4, 180, 768), BF16),
                pltpu.VMEM((768, 128), BF16),
                pltpu.VMEM((4, 32), jnp.int32),
                pltpu.VMEM((4, 180), jnp.int32),
                pltpu.VMEM((16, 128, 128), BF16),
                pltpu.VMEM((4, 2, 2, 2 * DPAD, 128), BF16),
                pltpu.VMEM((32, 2048), F32),
                pltpu.VMEM((16, 1, 128), F32),
                pltpu.VMEM((8, 1, 128), F32),
                pltpu.VMEM((16, 1, 128), F32),
                pltpu.VMEM((8, 1, 128), F32),
                dma((8,)), dma((16,)), dma((16,)), dma((6,)), dma((6,)), dma((8,)), dma((8,)),
                dma((16,)), dma((16,)), dma((8,)), dma((8,)), dma((16,)), dma((16,)), dma((8,)), dma((8,)),
            ],
            compiler_params=pltpu.CompilerParams(collective_id=0, has_side_effects=True,
                                                 vmem_limit_bytes=48 * 1024 * 1024),
        )(q_hidden, d_hidden, w_proj, q_mask, d_mask, temperature.reshape(1))
        return lq[0, :4], ld[0, :4], lm[0, :1]

    return jax.shard_map(local_loss, mesh=mesh, in_specs=(batch_spec, batch_spec, P(), batch_spec, batch_spec, P()),
                         out_specs=(batch_spec, batch_spec, P('replica')), check_vma=False)
```

time: 184 us -> 44.8 us (0.24)
  waiting for transfers between devices: 77.8 us -> 0 us
  blocking collectives: 62.8 us -> 0 us
  Pallas kernels: 0 us -> 40.2 us
  between operations: 16.6 us -> 2.57 us
  matrix products: 10.5 us -> 0 us
  starting transfers between devices: 5.34 us -> 0 us
  local copies, waits for them, and re-layouts: 6.77 us -> 1.89 us
  other arithmetic: 3.45 us -> 0 us
    all_gather x1 -> x0, waiting for transfers between devices: 68 us -> none  [local_loss(): q_group = lax.all_gather(q_vecs, 'data', tiled=True)]
    psum x1 -> x0, blocking collectives: 62.8 us -> none  [local_loss(): group_sum = lax.psum(jnp.sum(loss_query + loss_doc), 'data')]
    pallas_call x0 -> x1, Pallas kernels: none -> 40.2 us  [local_loss(): pl.pallas_call(kernel, out_shape=(out, out, out), in_specs=[any_spec] * 5...]
    dot_general x4 -> x0, matrix products: 10.5 us -> none  [the longest x2 7.47 us: maxsim(): jnp.einsum('itk,jsk->itjs', q_vecs, p_vecs, preferred_element_type=jnp.fl...]
    all_to_all x1 -> x0, waiting for transfers between devices: 9.72 us -> none  [local_loss(): row_scores = lax.all_to_all(col_scores, 'data', 0, 1, tiled=True)]
    all_to_all x1 -> x0, starting transfers between devices: 5.31 us -> none  [local_loss(): row_scores = lax.all_to_all(col_scores, 'data', 0, 1, tiled=True)]
    dynamic_slice x3 -> x0, local copies, waits for them, and re-layouts: 3.98 us -> none  [the longest x2 3.91 us: local_loss(): lax.map(functools.partial(maxsim, p_vecs=p_vecs, d_mask=d_mask), q_steps)]
  transfers between devices with their start and end apart: 2 -> 0, of which waited for: 2 -> 0; matrix products, arithmetic and copies ran while one was open for 2% -> 0% of each run, Pallas kernels for 0% -> 0%
where the time goes in v1:
time: 44.8 us; the launch traced here: 44.7 us
  Pallas kernels  40.2 us (90%)
  between operations  2.57 us (6%)
  local copies, waits for them, and re-layouts  1.89 us (4%)
    pallas_call x1, Pallas kernels, local_loss(): pl.pallas_call(kernel, out_shape=(out, out, out), in_specs=[any_spec] * 5...  40.2 us
    unnamed x9, local copies, waits for them, and re-layouts  1.38 us

profile of v1, /device:TPU:1, one launch (start us, length us, event | category | flops | bytes accessed | tf_op | source)
XLA Modules:
  0.0 44.7 jit_solution(2491668112271394274)
XLA Ops:
  0.6 0.0 copy-start.2
  0.6 0.0 copy-start.3
  0.7 0.0 copy-start.1
  0.7 0.0 copy-start
  1.4 1.4 %copy.9.d_hbm = bf16[4,180,768]{2,1,0:T(8,128)(2,1)S(1)} copy(bf16[4,180,768]{2,0,1:T(4,128)(2,1)} %param.7) | data formatting | bytes 2211840 | tf_op args[1]
  2.7 0.0 copy-done.2
  2.7 0.0 copy-done.3
  2.8 0.0 copy-done.1
  2.8 0.0 copy-done
  2.8 40.2 %shard_map.85 = (f32[1,128]{1,0:T(1,128)S(1)}, f32[1,128]{1,0:T(1,128)S(1)}, f32[1,128]{1,0:T(1,128)S(1)}) custom-call(bf16[4,32,768]{2,1,0:T(8,128)(2,1)S(1)} %copy-done, bf16[4,180,768]{2,1,0:T(8,128)(2,1)S(1)} %copy.9.d_hbm, bf16[768,128]{1,0:T(8,128)(2,1)S(1)} %copy-done.1, s32[4,32]{1,0:T(4,128)S(1)} %copy-done.3, s32[4,180]{1,0:T(4,128)S(1)} %copy-done.2, ...), custom_call_target="tpu_custom_call" | custom-call | tf_op jit(solution)/shard_map/pallas_call | solution.py:277
  43.0 0.5 %slice_bitcast_fusion = (f32[4]{0:T(128)}, f32[4]{0:T(128)}) fusion(f32[1,128]{1,0:T(1,128)S(1)} %get-tuple-element.7, f32[1,128]{1,0:T(1,128)S(1)} %get-tuple-element.6), kind=kLoop, calls=%fused_computation | loop fusion | bytes 64 | tf_op jit(solution)/shard_map/squeeze | solution.py:301
Async XLA Ops:
  0.6 2.1 %copy-start.2 = (s32[4,180]{1,0:T(4,128)S(1)}, s32[4,180]{1,0:T(4,128)}, u32[]{:S(2)}) copy-start(s32[4,180]{1,0:T(4,128)} %dm_hbm.1) | copy-start | bytes 8644
  0.6 2.1 %copy-start.3 = (s32[4,32]{1,0:T(4,128)S(1)}, s32[4,32]{1,0:T(4,128)}, u32[]{:S(2)}) copy-start(s32[4,32]{1,0:T(4,128)} %qm_hbm.1) | copy-start | bytes 1540
  0.7 2.1 %copy-start.1 = (bf16[768,128]{1,0:T(8,128)(2,1)S(1)}, bf16[768,128]{1,0:T(8,128)(2,1)}, u32[]{:S(2)}) copy-start(bf16[768,128]{1,0:T(8,128)(2,1)} %w_hbm.1) | copy-start | bytes 589828
  0.7 2.1 %copy-start = (bf16[4,32,768]{2,1,0:T(8,128)(2,1)S(1)}, bf16[4,32,768]{2,1,0:T(8,128)(2,1)}, u32[]{:S(2)}) copy-start(bf16[4,32,768]{2,1,0:T(8,128)(2,1)} %q_hbm.1) | copy-start | bytes 589828

commit v2 on v1

v2 whole, which is shorter than its diff:
```python
import jax
import jax.numpy as jnp
from jax import lax
from jax.experimental import pallas as pl
from jax.experimental.pallas import tpu as pltpu
from jax.sharding import PartitionSpec as P

F32 = jnp.float32
BF16 = jnp.bfloat16
MESH = pl.DeviceIdType.MESH
DPAD = 184
Q_ORDER = (0, 1, 3, 4, 12, 5, 7, 13, 15, 2, 8, 6, 14, 9, 11, 10)
OWN, LEFT, RIGHT, OPP = 0, 1, 2, 3


def unit_rows(raw):
    return raw / jnp.sqrt(jnp.sum(raw * raw, axis=-1, keepdims=True))


def iota(shape, axis):
    return lax.broadcasted_iota(jnp.int32, shape, axis)


def kernel(qh, dh, w, qm, dm, temp_ref, lq_ref, ld_ref, lm_ref,
           qbuf, dbuf, best, pick, rowbuf, colbuf, row2, col2,
           qs, qr, ds_, dr, ps, pr, rs, rr, cs, cr, rs2, rr2, cs2, cr2):
    me = lax.axis_index('data')
    c = lax.rem(me, 2)
    x = lax.rem(me // 2, 4)
    y = lax.rem(me // 8, 4)
    z = me // 32

    def dev(z_, y_, x_, c_):
        return {'data': ((z_ * 4 + y_) * 4 + x_) * 2 + c_}

    def plane(r):
        return lax.rem(z + r // 4, 4), lax.rem(y + r % 4, 4)

    def plane_back(r):
        return lax.rem(z + 4 - r // 4, 4), lax.rem(y + 4 - r % 4, 4)

    def line_back(r):
        return lax.rem(x + 4 - r // 2, 4), lax.rem(c + r % 2, 2)

    barrier = pltpu.get_barrier_semaphore()
    for r in Q_ORDER[1:]:
        zz, yy = plane_back(r)
        pl.semaphore_signal(barrier, inc=1, device_id=dev(zz, yy, x, c), device_id_type=MESH)
    for r in range(1, 8):
        xx, cc = line_back(r)
        pl.semaphore_signal(barrier, inc=1, device_id=dev(z, y, xx, cc), device_id_type=MESH)

    q_raw = jnp.dot(qh[...].reshape(128, 768), w[...], preferred_element_type=F32)
    q_col = jnp.transpose(jnp.concatenate([qm[...].astype(F32), jnp.zeros((4, 32), F32)], axis=0))
    q_valid = jnp.concatenate([q_col[:, i:i + 1] for i in range(4)], axis=0)
    qbuf[0] = jnp.where(q_valid == 1.0, unit_rows(q_raw), 0.0).astype(BF16)

    d_col = jnp.transpose(jnp.concatenate([dm[...].astype(F32), jnp.zeros((4, 180), F32)], axis=0))
    pos = iota((180, 1), 0)
    for h in range(2):
        parts = []
        for j in (2 * h, 2 * h + 1):
            u = unit_rows(jnp.dot(dh[j], w[...], preferred_element_type=F32))
            valid = d_col[:, j:j + 1] == 1.0
            first = jnp.min(jnp.where(valid, pos, 1000), axis=0, keepdims=True)
            vec = jnp.sum(jnp.where(pos == first, u, 0.0), axis=0, keepdims=True)
            parts += [jnp.where(valid, u, vec), jnp.broadcast_to(vec, (DPAD - 180, 128))]
        dbuf[OWN, 0, h] = jnp.concatenate(parts, axis=0).astype(BF16)

    def plane_slot(r):
        zz, yy = plane(r)
        return zz * 4 + yy

    tok = iota((128, 128), 0) // 32
    lanes = iota((128, 128), 1)
    for p in range(16):
        pick[p * 128:(p + 1) * 128, :] = (tok + 4 * plane_slot(Q_ORDER[p]) == lanes).astype(F32).astype(BF16)

    pl.semaphore_wait(barrier, 22)

    xr, xl = lax.rem(x + 1, 4), lax.rem(x + 3, 4)
    right, left, partner = dev(z, y, xr, c), dev(z, y, xl, c), dev(z, y, x, 1 - c)
    sends = []

    def rdma(src, dst, ssem, rsem, to):
        return pltpu.make_async_remote_copy(src, dst, ssem, rsem, device_id=to, device_id_type=MESH)

    def send(cp):
        cp.start()
        sends.append(cp)

    ICI = [(LEFT, 0), (LEFT, 1), (RIGHT, 0), (RIGHT, 1), (OPP, 0), (OPP, 1)]

    def to_right(src, h, i):
        return rdma(dbuf.at[src, 0, h], dbuf.at[ICI[i][0], 0, h], ds_.at[i], dr.at[i], right)

    def to_left(src, h, i):
        return rdma(dbuf.at[src, 0, h], dbuf.at[ICI[i][0], 0, h], ds_.at[i], dr.at[i], left)

    def to_partner(src, h):
        return rdma(dbuf.at[src, 0, h], dbuf.at[src, 1, h], ps.at[2 * src + h], pr.at[2 * src + h], partner)

    def q_copy(p):
        zz, yy = plane_back(Q_ORDER[p])
        return rdma(qbuf.at[0], qbuf.at[p], qs.at[p], qr.at[p], dev(zz, yy, x, c))

    for h in range(2):
        send(to_right(OWN, h, h))
        send(to_left(OWN, h, 2 + h))
        send(to_partner(OWN, h))
    for p in range(1, 16):
        send(q_copy(p))

    def wait_ici(i):
        side, h = ICI[i]
        to_right(OWN, h, i).wait_recv()
        if i == 0:
            send(to_right(LEFT, 0, 4))
        if i == 3:
            send(to_left(RIGHT, 1, 5))
        send(to_partner(side, h))

    def wait_partner(side, h):
        to_partner(side, h).wait_recv()

    def wait_q(k):
        for p in range(max(1, 4 * k), 4 * k + 4):
            q_copy(p).wait_recv()

    def block(pieces, chunks):
        n = len(pieces)
        lhs = jnp.concatenate([dbuf[piece] for piece in pieces], axis=0)
        for k in chunks:
            rhs = qbuf[4 * k:4 * k + 4].reshape(512, 128)
            sim = lax.dot_general(lhs, rhs, (((1,), (1,)), ((), ())), preferred_element_type=F32)
            top = jnp.max(sim.reshape(2 * n, DPAD, 512), axis=1)
            for i, (side, core, h) in enumerate(pieces):
                row = side * 8 + core * 4 + h * 2
                best[row:row + 2, k * 512:(k + 1) * 512] = top[2 * i:2 * i + 2]

    own = [(OWN, a, h) for a in range(2) for h in range(2)]
    near0 = [(s, a, 0) for s in (LEFT, RIGHT) for a in range(2)]
    near1 = [(s, a, 1) for s in (LEFT, RIGHT) for a in range(2)]
    opp = [(OPP, a, h) for a in range(2) for h in range(2)]

    wait_partner(OWN, 0)
    wait_partner(OWN, 1)
    wait_q(0)
    block(own, [0])
    wait_ici(0)
    wait_ici(2)
    wait_q(1)
    block(own, [1])
    wait_ici(1)
    wait_ici(3)
    wait_partner(LEFT, 0)
    wait_partner(RIGHT, 0)
    wait_q(2)
    block(own, [2])
    block(near0, [0, 1, 2])
    wait_ici(4)
    wait_ici(5)
    wait_partner(LEFT, 1)
    wait_partner(RIGHT, 1)
    block(near1, [0, 1, 2])
    wait_q(3)
    block(own, [3])
    block(near0, [3])
    block(near1, [3])
    wait_partner(OPP, 0)
    wait_partner(OPP, 1)
    block(opp, [0, 1, 2, 3])

    b = best[...]
    hi = b.astype(BF16)
    rest = b - hi.astype(F32)
    mid = rest.astype(BF16)
    low = (rest - mid.astype(F32)).astype(BF16)
    sums = jnp.dot(jnp.concatenate([hi, mid, low], axis=0), pick[...], preferred_element_type=F32)
    logits = ((sums[0:32] + sums[32:64]) + sums[64:96]) / temp_ref[0]
    lane = iota((32, 128), 1)
    sub = iota((32, 128), 0)
    lane1 = iota((1, 128), 1)
    my_slot = z * 4 + y
    my_line = x * 2 + c
    mine = (sub < 4) & (lane - my_slot * 4 == sub)
    pos_q = jnp.sum(jnp.where(mine, logits, 0.0), axis=0, keepdims=True)
    pos_total = jnp.sum(pos_q, axis=1, keepdims=True)
    m_row = jnp.max(logits, axis=0, keepdims=True)
    l_row = jnp.sum(jnp.exp(logits - m_row), axis=0, keepdims=True)
    qlane = lane < 64
    m_col = jnp.max(jnp.where(qlane, logits, -jnp.inf), axis=1, keepdims=True)
    l_col = jnp.sum(jnp.where(qlane, jnp.exp(logits - m_col), 0.0), axis=1, keepdims=True)
    side = sub // 8
    off = jnp.where(side == LEFT, 3, jnp.where(side == RIGHT, 1, jnp.where(side == OPP, 2, 0)))
    doc = ((x + off) & 3) * 8 + ((c + sub // 4) & 1) * 4 + (sub & 3)
    m_colr = jnp.sum(jnp.where(doc == lane, m_col, 0.0), axis=0, keepdims=True)
    l_colr = jnp.sum(jnp.where(doc == lane - 32, l_col, 0.0), axis=0, keepdims=True)
    rowbuf[my_slot] = jnp.where(lane1 < 64, m_row, pltpu.roll(l_row, 64, 1))
    colbuf[my_line] = jnp.where(lane1 == 64, pos_total, m_colr + l_colr)

    def plane_copy(buf, r, ss, rs_):
        zz, yy = plane_back(r)
        return rdma(buf.at[my_slot], buf.at[my_slot], ss.at[r], rs_.at[r], dev(zz, yy, x, c))

    def line_copy(buf, r, ss, rs_):
        xx, cc = line_back(r)
        return rdma(buf.at[my_line], buf.at[my_line], ss.at[r], rs_.at[r], dev(z, y, xx, cc))

    far_first = Q_ORDER[:0:-1]
    rows1 = [plane_copy(rowbuf, r, rs, rr) for r in far_first]
    cols1 = [line_copy(colbuf, r, cs, cr) for r in (5, 4, 3, 7, 2, 6, 1)]
    for cp in rows1 + cols1:
        cp.start()
    for cp in cols1 + rows1:
        cp.wait_recv()
    rb = rowbuf[...].reshape(16, 128)
    rb_l = pltpu.roll(rb, 64, 1)
    m = jnp.max(rb, axis=0, keepdims=True)
    lse_row = m + jnp.log(jnp.sum(rb_l * jnp.exp(rb - m), axis=0, keepdims=True))
    row_total = jnp.sum(jnp.where(lane1 < 64, lse_row, 0.0), axis=1, keepdims=True)
    cb = colbuf[...].reshape(8, 128)
    cb_l = pltpu.roll(cb, 96, 1)
    mc = jnp.max(cb, axis=0, keepdims=True)
    lse_col = mc + jnp.log(jnp.sum(cb_l * jnp.exp(cb - mc), axis=0, keepdims=True))
    col_total = jnp.sum(jnp.where(lane1 < 32, lse_col, 0.0), axis=1, keepdims=True)
    pos_sum = jnp.sum(jnp.sum(jnp.where(lane1 == 64, cb, 0.0), axis=0, keepdims=True), axis=1, keepdims=True)
    row2[my_slot] = jnp.broadcast_to(col_total - 2.0 * pos_sum, (1, 128))
    col2[my_line] = jnp.broadcast_to(row_total, (1, 128))
    rows2 = [plane_copy(row2, r, rs2, rr2) for r in far_first]
    cols2 = [line_copy(col2, r, cs2, cr2) for r in (5, 4, 3, 7, 2, 6, 1)]
    for cp in rows2 + cols2:
        cp.start()

    def to_front(v, start):
        return pltpu.roll(v, lax.rem(128 - start, 128), 1)

    pos_front = to_front(pos_q, my_slot * 4)
    lq_ref[...] = (to_front(lse_row, my_slot * 4) - pos_front)[0, :4]
    ld_ref[...] = (to_front(lse_col, my_line * 4) - pos_front)[0, :4]
    for cp in sends + rows1 + cols1:
        cp.wait_send()
    for cp in cols2 + rows2:
        cp.wait_recv()
    total = (jnp.sum(row2[...].reshape(16, 128), axis=0, keepdims=True)
             + jnp.sum(col2[...].reshape(8, 128), axis=0, keepdims=True))
    lm_ref[...] = (total / 1024.0)[0, :1]
    for cp in rows2 + cols2:
        cp.wait_send()


def solution(mesh):
    batch_spec = P(('replica', 'data'))

    def local_loss(q_hidden, d_hidden, w_proj, q_mask, d_mask, temperature):
        vmem = pl.BlockSpec(memory_space=pltpu.VMEM)
        dma = pltpu.SemaphoreType.DMA
        return pl.pallas_call(
            kernel,
            out_shape=tuple(jax.ShapeDtypeStruct((n,), F32) for n in (4, 4, 1)),
            in_specs=[vmem] * 5 + [pl.BlockSpec(memory_space=pltpu.SMEM)],
            out_specs=(vmem, vmem, vmem),
            scratch_shapes=[
                pltpu.VMEM((16, 128, 128), BF16),
                pltpu.VMEM((4, 2, 2, 2 * DPAD, 128), BF16),
                pltpu.VMEM((32, 2048), F32),
                pltpu.VMEM((2048, 128), BF16),
                pltpu.VMEM((16, 1, 128), F32),
                pltpu.VMEM((8, 1, 128), F32),
                pltpu.VMEM((16, 1, 128), F32),
                pltpu.VMEM((8, 1, 128), F32),
                dma((16,)), dma((16,)), dma((6,)), dma((6,)), dma((8,)), dma((8,)),
                dma((16,)), dma((16,)), dma((8,)), dma((8,)), dma((16,)), dma((16,)), dma((8,)), dma((8,)),
            ],
            compiler_params=pltpu.CompilerParams(collective_id=0, has_side_effects=True,
                                                 vmem_limit_bytes=48 * 1024 * 1024),
        )(q_hidden, d_hidden, w_proj, q_mask, d_mask, temperature.reshape(1))

    return jax.shard_map(local_loss, mesh=mesh, in_specs=(batch_spec, batch_spec, P(), batch_spec, batch_spec, P()),
                         out_specs=(batch_spec, batch_spec, P('replica')), check_vma=False)
```

time: 44.8 us -> 39.9 us (0.89)
  Pallas kernels: 40.2 us -> 34.2 us
  between operations: 2.57 us -> 3.15 us
  local copies, waits for them, and re-layouts: 1.89 us -> 2.4 us
    pallas_call x1, Pallas kernels: 40.2 us -> 34.2 us  [local_loss(): pl.pallas_call(kernel, out_shape=tuple((jax.ShapeDtypeStruct((n,), F32) f...]
    unnamed x9 -> x11, local copies, waits for them, and re-layouts: 1.38 us -> 2.4 us
    squeeze x1 -> x0, local copies, waits for them, and re-layouts: 0.52 us -> none  [local_loss(): return (lq[0, :4], ld[0, :4], lm[0, :1])]
where the time goes in v2:
time: 39.9 us; the launch traced here: 39.8 us
  Pallas kernels  34.2 us (86%)
  between operations  3.15 us (8%)
  local copies, waits for them, and re-layouts  2.4 us (6%)
    pallas_call x1, Pallas kernels, local_loss(): pl.pallas_call(kernel, out_shape=tuple((jax.ShapeDtypeStruct((n,), F32) f...  34.2 us
    unnamed x11, local copies, waits for them, and re-layouts  2.4 us

profile of v2, /device:TPU:1, one launch (start us, length us, event | category | flops | bytes accessed | tf_op | source)
XLA Modules:
  0.0 39.8 jit_solution(10387156065942585847)
XLA Ops:
  0.6 0.0 copy-start.2
  0.6 0.0 copy-start.3
  0.7 0.0 copy-start.1
  0.7 0.0 copy-start
  1.4 1.4 %copy.9.dh = bf16[4,180,768]{2,1,0:T(8,128)(2,1)S(1)} copy(bf16[4,180,768]{2,0,1:T(4,128)(2,1)} %param.7) | data formatting | bytes 2211840 | tf_op args[1]
  2.7 0.0 copy-done.2
  2.7 0.0 copy-done.3
  2.8 0.0 copy-done.1
  2.8 0.0 copy-done
  2.8 34.2 %shard_map.85 = (f32[4]{0:T(128)S(1)}, f32[4]{0:T(128)S(1)}, f32[1]{0:T(128)}) custom-call(bf16[4,32,768]{2,1,0:T(8,128)(2,1)S(1)} %copy-done, bf16[4,180,768]{2,1,0:T(8,128)(2,1)S(1)} %copy.9.dh, bf16[768,128]{1,0:T(8,128)(2,1)S(1)} %copy-done.1, s32[4,32]{1,0:T(4,128)S(1)} %copy-done.3, s32[4,180]{1,0:T(4,128)S(1)} %copy-done.2, f32[1]{0:T(128)} %bitcast.1.temp_ref), custom_call_target="tpu_custom_call" | custom-call | tf_op jit(solution)/shard_map/pallas_call | solution.py:258
  37.0 0.5 %copy.14 = f32[4]{0:T(128)} copy(f32[4]{0:T(128)S(1)} %get-tuple-element.6) | data formatting | bytes 32
  37.5 0.5 %copy.15 = f32[4]{0:T(128)} copy(f32[4]{0:T(128)S(1)} %get-tuple-element.7) | data formatting | bytes 32
Async XLA Ops:
  0.6 2.1 %copy-start.2 = (s32[4,180]{1,0:T(4,128)S(1)}, s32[4,180]{1,0:T(4,128)}, u32[]{:S(2)}) copy-start(s32[4,180]{1,0:T(4,128)} %dm.1) | copy-start | bytes 8644
  0.6 2.1 %copy-start.3 = (s32[4,32]{1,0:T(4,128)S(1)}, s32[4,32]{1,0:T(4,128)}, u32[]{:S(2)}) copy-start(s32[4,32]{1,0:T(4,128)} %qm.1) | copy-start | bytes 1540
  0.7 2.1 %copy-start.1 = (bf16[768,128]{1,0:T(8,128)(2,1)S(1)}, bf16[768,128]{1,0:T(8,128)(2,1)}, u32[]{:S(2)}) copy-start(bf16[768,128]{1,0:T(8,128)(2,1)} %w.1) | copy-start | bytes 589828
  0.7 2.1 %copy-start = (bf16[4,32,768]{2,1,0:T(8,128)(2,1)S(1)}, bf16[4,32,768]{2,1,0:T(8,128)(2,1)}, u32[]{:S(2)}) copy-start(bf16[4,32,768]{2,1,0:T(8,128)(2,1)} %qh.1) | copy-start | bytes 589828

commit v3 on v2

v3 whole, which is shorter than its diff:
```python
import jax
import jax.numpy as jnp
from jax import lax
from jax.experimental import pallas as pl
from jax.experimental.pallas import tpu as pltpu
from jax.sharding import PartitionSpec as P

F32 = jnp.float32
BF16 = jnp.bfloat16
MESH = pl.DeviceIdType.MESH
DPAD = 184
Q_ORDER = (0, 1, 3, 4, 12, 2, 8, 5, 7, 13, 15, 6, 14, 9, 11, 10)
P_Y2, P_Z2, P_FAR = 5, 6, 11
OWN, LEFT, RIGHT, OPP = 0, 1, 2, 3


def unit_rows(raw):
    return raw / jnp.sqrt(jnp.sum(raw * raw, axis=-1, keepdims=True))


def iota(shape, axis):
    return lax.broadcasted_iota(jnp.int32, shape, axis)


def kernel(qh, dh, w, qm, dm, temp_ref, lq_ref, ld_ref, lm_ref,
           qbuf, dbuf, best, pick, part, qs, qr, ds_, dr, ps, pr, fs, fr, ready):
    me = lax.axis_index('data')
    c = lax.rem(me, 2)
    x = lax.rem(me // 2, 4)
    y = lax.rem(me // 8, 4)
    z = me // 32

    def dev(z_, y_, x_, c_):
        return {'data': ((z_ * 4 + y_) * 4 + x_) * 2 + c_}

    def plane(r):
        return lax.rem(z + r // 4, 4), lax.rem(y + r % 4, 4)

    def plane_back(r):
        return lax.rem(z + 4 - r // 4, 4), lax.rem(y + 4 - r % 4, 4)

    def line_back(r):
        return lax.rem(x + 4 - r // 2, 4), lax.rem(c + r % 2, 2)

    barrier = pltpu.get_barrier_semaphore()
    for r in Q_ORDER[1:P_FAR]:
        zz, yy = plane_back(r)
        pl.semaphore_signal(barrier, inc=1, device_id=dev(zz, yy, x, c), device_id_type=MESH)
    for r in range(1, 8):
        xx, cc = line_back(r)
        pl.semaphore_signal(barrier, inc=1, device_id=dev(z, y, xx, cc), device_id_type=MESH)

    q_raw = jnp.dot(qh[...].reshape(128, 768), w[...], preferred_element_type=F32)
    q_col = jnp.transpose(jnp.concatenate([qm[...].astype(F32), jnp.zeros((4, 32), F32)], axis=0))
    q_valid = jnp.concatenate([q_col[:, i:i + 1] for i in range(4)], axis=0)
    qbuf[0] = jnp.where(q_valid == 1.0, unit_rows(q_raw), 0.0).astype(BF16)

    d_col = jnp.transpose(jnp.concatenate([dm[...].astype(F32), jnp.zeros((4, 180), F32)], axis=0))
    pos = iota((180, 1), 0)
    for h in range(2):
        parts = []
        for j in (2 * h, 2 * h + 1):
            u = unit_rows(jnp.dot(dh[j], w[...], preferred_element_type=F32))
            valid = d_col[:, j:j + 1] == 1.0
            first = jnp.min(jnp.where(valid, pos, 1000), axis=0, keepdims=True)
            vec = jnp.sum(jnp.where(pos == first, u, 0.0), axis=0, keepdims=True)
            parts += [jnp.where(valid, u, vec), jnp.broadcast_to(vec, (DPAD - 180, 128))]
        dbuf[OWN, 0, h] = jnp.concatenate(parts, axis=0).astype(BF16)

    pl.semaphore_wait(barrier, 17)

    xr, xl = lax.rem(x + 1, 4), lax.rem(x + 3, 4)
    right, left, partner = dev(z, y, xr, c), dev(z, y, xl, c), dev(z, y, x, 1 - c)
    sends = []

    def rdma(src, dst, ssem, rsem, to):
        return pltpu.make_async_remote_copy(src, dst, ssem, rsem, device_id=to, device_id_type=MESH)

    def send(cp):
        cp.start()
        sends.append(cp)

    ICI = [(LEFT, 0), (RIGHT, 1), (LEFT, 1), (RIGHT, 0), (OPP, 0), (OPP, 1)]

    def to_right(src, h, i):
        return rdma(dbuf.at[src, 0, h], dbuf.at[ICI[i][0], 0, h], ds_.at[i], dr.at[i], right)

    def to_left(src, h, i):
        return rdma(dbuf.at[src, 0, h], dbuf.at[ICI[i][0], 0, h], ds_.at[i], dr.at[i], left)

    def to_partner(src, h):
        return rdma(dbuf.at[src, 0, h], dbuf.at[src, 1, h], ps.at[2 * src + h], pr.at[2 * src + h], partner)

    def q_copy(p):
        dz, dy = Q_ORDER[p] // 4, Q_ORDER[p] % 4
        src = 0
        if p >= P_FAR:
            if dy == 2:
                src, dy = P_Y2, 0
            else:
                src, dz = P_Z2, 0
        zz, yy = plane_back(4 * dz + dy)
        return rdma(qbuf.at[src], qbuf.at[p], qs.at[p], qr.at[p], dev(zz, yy, x, c))

    send(to_right(OWN, 0, 0))
    send(to_left(OWN, 1, 1))
    for p in (P_Y2, P_Z2, 1, 2, 3, 4):
        send(q_copy(p))
    send(to_partner(OWN, 0))
    send(to_partner(OWN, 1))
    send(to_right(OWN, 1, 2))
    send(to_left(OWN, 0, 3))
    for p in range(P_Z2 + 1, P_FAR):
        send(q_copy(p))

    def plane_slot(r):
        zz, yy = plane(r)
        return zz * 4 + yy

    tok = iota((128, 128), 0) // 32
    lanes = iota((128, 128), 1)
    for p in range(16):
        pick[p * 128:(p + 1) * 128, :] = (tok + 4 * plane_slot(Q_ORDER[p]) == lanes).astype(F32).astype(BF16)

    def wait_ici(i):
        side, h = ICI[i]
        to_right(OWN, h, i).wait_recv()
        if i == 0:
            send(to_right(LEFT, 0, 4))
        if i == 1:
            send(to_left(RIGHT, 1, 5))
        send(to_partner(side, h))

    def wait_partner(side, h):
        to_partner(side, h).wait_recv()

    def wait_q(*blocks):
        for p in blocks:
            q_copy(p).wait_recv()

    def block(pieces, chunks):
        n = len(pieces)
        lhs = jnp.concatenate([dbuf[piece] for piece in pieces], axis=0)
        for k in chunks:
            rhs = qbuf[4 * k:4 * k + 4].reshape(512, 128)
            sim = lax.dot_general(lhs, rhs, (((1,), (1,)), ((), ())), preferred_element_type=F32)
            top = jnp.max(sim.reshape(2 * n, DPAD, 512), axis=1)
            for i, (side, core, h) in enumerate(pieces):
                row = side * 8 + core * 4 + h * 2
                best[row:row + 2, k * 512:(k + 1) * 512] = top[2 * i:2 * i + 2]

    def group(side, h):
        return [(side, a, h) for a in range(2)]

    own = group(OWN, 0) + group(OWN, 1)
    near0 = group(LEFT, 0) + group(RIGHT, 1)
    near1 = group(LEFT, 1) + group(RIGHT, 0)

    wait_partner(OWN, 0)
    wait_partner(OWN, 1)
    wait_q(1, 2, 3)
    block(own, [0])
    wait_q(P_Y2, P_Z2)
    for p in range(P_FAR, 16):
        send(q_copy(p))
    wait_ici(0)
    wait_ici(1)
    wait_q(4, 7)
    block(own, [1])
    wait_ici(2)
    wait_ici(3)
    wait_partner(LEFT, 0)
    wait_partner(RIGHT, 1)
    block(near0, [0, 1])
    wait_q(8, 9, 10, 11)
    block(own, [2])
    block(near0, [2])
    wait_partner(LEFT, 1)
    wait_partner(RIGHT, 0)
    wait_ici(4)
    wait_ici(5)
    wait_q(12, 13, 14, 15)
    for r in range(1, 16):
        zz, yy = plane_back(r)
        pl.semaphore_signal(ready, inc=1, device_id=dev(zz, yy, x, c), device_id_type=MESH)
    block(near1, [0, 1, 2])
    block(own, [3])
    block(near0, [3])
    block(near1, [3])
    block([(OPP, 0, 0), (OPP, 0, 1)], [0, 1, 2, 3])
    wait_partner(OPP, 0)
    wait_partner(OPP, 1)
    block([(OPP, 1, 0), (OPP, 1, 1)], [0, 1, 2, 3])

    b = best[...]
    hi = b.astype(BF16)
    rest = b - hi.astype(F32)
    mid = rest.astype(BF16)
    low = (rest - mid.astype(F32)).astype(BF16)
    sums = jnp.dot(jnp.concatenate([hi, mid, low], axis=0), pick[...], preferred_element_type=F32)
    logits = ((sums[0:32] + sums[32:64]) + sums[64:96]) / temp_ref[0]
    lane = iota((32, 128), 1)
    sub = iota((32, 128), 0)
    lane1 = iota((1, 128), 1)
    my_slot = z * 4 + y
    my_line = x * 2 + c
    mine = (sub < 4) & (lane - my_slot * 4 == sub)
    pos_q = jnp.sum(jnp.where(mine, logits, 0.0), axis=0, keepdims=True)
    pos_total = jnp.sum(pos_q, axis=1, keepdims=True)
    m_row = jnp.max(logits, axis=0, keepdims=True)
    l_row = jnp.sum(jnp.exp(logits - m_row), axis=0, keepdims=True)
    qlane = lane < 64
    m_col = jnp.max(jnp.where(qlane, logits, -jnp.inf), axis=1, keepdims=True)
    l_col = jnp.sum(jnp.where(qlane, jnp.exp(logits - m_col), 0.0), axis=1, keepdims=True)
    side = sub // 8
    off = jnp.where(side == LEFT, 3, jnp.where(side == RIGHT, 1, jnp.where(side == OPP, 2, 0)))
    doc = ((x + off) & 3) * 8 + ((c + sub // 4) & 1) * 4 + (sub & 3)
    m_colr = jnp.sum(jnp.where(doc == lane - 64, m_col, 0.0), axis=0, keepdims=True)
    l_colr = jnp.sum(jnp.where(doc == lane - 64, l_col, 0.0), axis=0, keepdims=True)
    top_row = jnp.where(lane1 < 64, m_row, jnp.where(lane1 == 96, pos_total, m_colr))
    sum_row = jnp.where(lane1 < 64, l_row, l_colr)
    part[me] = jnp.concatenate([top_row, sum_row], axis=0)
    pl.semaphore_wait(ready, 15)

    def hops(r):
        return sum((0, 1, 2, 1)[(r >> b) & 3] for b in (1, 3, 5))

    for r in sorted(range(1, 128), key=hops, reverse=True):
        rdma(part.at[me], part.at[me], fs, fr, {'data': me ^ r}).start()
    for cp in sends:
        cp.wait_send()
    everyone = rdma(part.at[0:127], part.at[0:127], fs, fr, partner)
    everyone.wait_recv()
    tops = part[:, 0, :].reshape(16, 8, 128)
    adds = part[:, 1, :].reshape(16, 8, 128)
    mr = jnp.max(tops, axis=0)
    lse_row = mr + jnp.log(jnp.sum(adds * jnp.exp(tops - mr[None]), axis=0))
    mc = jnp.max(tops, axis=1, keepdims=True)
    lse_col = (mc + jnp.log(jnp.sum(adds * jnp.exp(tops - mc), axis=1, keepdims=True))).reshape(16, 128)
    lane8 = iota((8, 128), 1)
    lane16 = iota((16, 128), 1)
    row_sum = jnp.sum(jnp.where(lane8 < 64, lse_row, 0.0), axis=0, keepdims=True)
    col_sum = jnp.sum(jnp.where((lane16 >= 64) & (lane16 < 96), lse_col, 0.0), axis=0, keepdims=True)
    pos_sum = jnp.sum(jnp.sum(tops, axis=0), axis=0, keepdims=True)
    total = jnp.sum(row_sum + col_sum - jnp.where(lane1 == 96, 2.0 * pos_sum, 0.0), axis=1, keepdims=True)
    lm_ref[...] = (total / 1024.0)[0, :1]

    def to_front(v, start):
        return pltpu.roll(v, lax.rem(128 - start, 128), 1)

    pos_front = to_front(pos_q, my_slot * 4)
    my_row = jnp.sum(jnp.where(iota((8, 128), 0) == my_line, lse_row, 0.0), axis=0, keepdims=True)
    my_col = jnp.sum(jnp.where(iota((16, 128), 0) == my_slot, lse_col, 0.0), axis=0, keepdims=True)
    lq_ref[...] = (to_front(my_row, my_slot * 4) - pos_front)[0, :4]
    ld_ref[...] = (to_front(my_col, 64 + my_line * 4) - pos_front)[0, :4]
    everyone.wait_send()


def solution(mesh):
    batch_spec = P(('replica', 'data'))

    def local_loss(q_hidden, d_hidden, w_proj, q_mask, d_mask, temperature):
        vmem = pl.BlockSpec(memory_space=pltpu.VMEM)
        dma = pltpu.SemaphoreType.DMA
        return pl.pallas_call(
            kernel,
            out_shape=tuple(jax.ShapeDtypeStruct((n,), F32) for n in (4, 4, 1)),
            in_specs=[vmem] * 5 + [pl.BlockSpec(memory_space=pltpu.SMEM)],
            out_specs=(vmem, vmem, vmem),
            scratch_shapes=[
                pltpu.VMEM((16, 128, 128), BF16),
                pltpu.VMEM((4, 2, 2, 2 * DPAD, 128), BF16),
                pltpu.VMEM((32, 2048), F32),
                pltpu.VMEM((2048, 128), BF16),
                pltpu.VMEM((128, 2, 128), F32),
                dma((16,)), dma((16,)), dma((6,)), dma((6,)), dma((8,)), dma((8,)), dma, dma,
                pltpu.SemaphoreType.REGULAR,
            ],
            compiler_params=pltpu.CompilerParams(collective_id=0, has_side_effects=True,
                                                 vmem_limit_bytes=48 * 1024 * 1024),
        )(q_hidden, d_hidden, w_proj, q_mask, d_mask, temperature.reshape(1))

    return jax.shard_map(local_loss, mesh=mesh, in_specs=(batch_spec, batch_spec, P(), batch_spec, batch_spec, P()),
                         out_specs=(batch_spec, batch_spec, P('replica')), check_vma=False)
```

time: 39.9 us -> 35.6 us (0.89)
  Pallas kernels: 34.2 us -> 29.9 us
    pallas_call x1, Pallas kernels: 34.2 us -> 29.9 us  [local_loss(): pl.pallas_call(kernel, out_shape=tuple((jax.ShapeDtypeStruct((n,), F32) f...]
where the time goes in v3:
time: 35.6 us; the launch traced here: 35.4 us
  Pallas kernels  29.9 us (84%)
  between operations  3.15 us (9%)
  local copies, waits for them, and re-layouts  2.4 us (7%)
    pallas_call x1, Pallas kernels, local_loss(): pl.pallas_call(kernel, out_shape=tuple((jax.ShapeDtypeStruct((n,), F32) f...  29.9 us
    unnamed x11, local copies, waits for them, and re-layouts  2.4 us

profile of v3, /device:TPU:1, one launch (start us, length us, event | category | flops | bytes accessed | tf_op | source)
XLA Modules:
  0.0 35.4 jit_solution(767591558532618392)
XLA Ops:
  0.6 0.0 copy-start.2
  0.6 0.0 copy-start.3
  0.7 0.0 copy-start.1
  0.7 0.0 copy-start
  1.4 1.4 %copy.9.dh = bf16[4,180,768]{2,1,0:T(8,128)(2,1)S(1)} copy(bf16[4,180,768]{2,0,1:T(4,128)(2,1)} %param.7) | data formatting | bytes 2211840 | tf_op args[1]
  2.7 0.0 copy-done.2
  2.7 0.0 copy-done.3
  2.8 0.0 copy-done.1
  2.8 0.0 copy-done
  2.8 29.9 %shard_map.85 = (f32[4]{0:T(128)S(1)}, f32[4]{0:T(128)S(1)}, f32[1]{0:T(128)}) custom-call(bf16[4,32,768]{2,1,0:T(8,128)(2,1)S(1)} %copy-done, bf16[4,180,768]{2,1,0:T(8,128)(2,1)S(1)} %copy.9.dh, bf16[768,128]{1,0:T(8,128)(2,1)S(1)} %copy-done.1, s32[4,32]{1,0:T(4,128)S(1)} %copy-done.3, s32[4,180]{1,0:T(4,128)S(1)} %copy-done.2, f32[1]{0:T(128)} %bitcast.1.temp_ref), custom_call_target="tpu_custom_call" | custom-call | tf_op jit(solution)/shard_map/pallas_call | solution.py:265
  32.7 0.5 %copy.14 = f32[4]{0:T(128)} copy(f32[4]{0:T(128)S(1)} %get-tuple-element.6) | data formatting | bytes 32
  33.2 0.5 %copy.15 = f32[4]{0:T(128)} copy(f32[4]{0:T(128)S(1)} %get-tuple-element.7) | data formatting | bytes 32
Async XLA Ops:
  0.6 2.1 %copy-start.2 = (s32[4,180]{1,0:T(4,128)S(1)}, s32[4,180]{1,0:T(4,128)}, u32[]{:S(2)}) copy-start(s32[4,180]{1,0:T(4,128)} %dm.1) | copy-start | bytes 8644
  0.6 2.1 %copy-start.3 = (s32[4,32]{1,0:T(4,128)S(1)}, s32[4,32]{1,0:T(4,128)}, u32[]{:S(2)}) copy-start(s32[4,32]{1,0:T(4,128)} %qm.1) | copy-start | bytes 1540
  0.7 2.1 %copy-start.1 = (bf16[768,128]{1,0:T(8,128)(2,1)S(1)}, bf16[768,128]{1,0:T(8,128)(2,1)}, u32[]{:S(2)}) copy-start(bf16[768,128]{1,0:T(8,128)(2,1)} %w.1) | copy-start | bytes 589828
  0.7 2.1 %copy-start = (bf16[4,32,768]{2,1,0:T(8,128)(2,1)S(1)}, bf16[4,32,768]{2,1,0:T(8,128)(2,1)}, u32[]{:S(2)}) copy-start(bf16[4,32,768]{2,1,0:T(8,128)(2,1)} %qh.1) | copy-start | bytes 589828

commit v4 on v3

--- a/solution.py
+++ b/solution.py
@@ -141,56 +141,60 @@
     def block(pieces, chunks):
         n = len(pieces)
         lhs = jnp.concatenate([dbuf[piece] for piece in pieces], axis=0)
-        for k in chunks:
-            rhs = qbuf[4 * k:4 * k + 4].reshape(512, 128)
+        for lo, hi in chunks:
+            width = (hi - lo) * 128
+            rhs = qbuf[lo:hi].reshape(width, 128)
             sim = lax.dot_general(lhs, rhs, (((1,), (1,)), ((), ())), preferred_element_type=F32)
-            top = jnp.max(sim.reshape(2 * n, DPAD, 512), axis=1)
+            top = jnp.max(sim.reshape(2 * n, DPAD, width), axis=1)
             for i, (side, core, h) in enumerate(pieces):
                 row = side * 8 + core * 4 + h * 2
-                best[row:row + 2, k * 512:(k + 1) * 512] = top[2 * i:2 * i + 2]
-
-    def group(side, h):
-        return [(side, a, h) for a in range(2)]
-
-    own = group(OWN, 0) + group(OWN, 1)
-    near0 = group(LEFT, 0) + group(RIGHT, 1)
-    near1 = group(LEFT, 1) + group(RIGHT, 0)
+                best[row:row + 2, lo * 128:hi * 128] = top[2 * i:2 * i + 2]
+
+    def pair(core, *halves):
+        return [(side, core, h) for side, h in halves]
+
+    own = pair(0, (OWN, 0), (OWN, 1)) + pair(1, (OWN, 0), (OWN, 1))
+    near0 = [pair(a, (LEFT, 0), (RIGHT, 1)) for a in range(2)]
+    near1 = [pair(a, (LEFT, 1), (RIGHT, 0)) for a in range(2)]
+    opp = [pair(a, (OPP, 0), (OPP, 1)) for a in range(2)]
+    A, B, C, D = (0, 4), (4, 8), (8, 10), (10, 16)
 
     wait_partner(OWN, 0)
     wait_partner(OWN, 1)
     wait_q(1, 2, 3)
-    block(own, [0])
+    block(own, [A])
     wait_q(P_Y2, P_Z2)
     for p in range(P_FAR, 16):
         send(q_copy(p))
     wait_ici(0)
     wait_ici(1)
+    block(near0[0], [A])
     wait_q(4, 7)
-    block(own, [1])
+    block(own, [B])
+    block(near0[0], [B])
+    wait_partner(LEFT, 0)
+    wait_partner(RIGHT, 1)
+    block(near0[1], [A, B])
     wait_ici(2)
     wait_ici(3)
-    wait_partner(LEFT, 0)
-    wait_partner(RIGHT, 1)
-    block(near0, [0, 1])
-    wait_q(8, 9, 10, 11)
-    block(own, [2])
-    block(near0, [2])
+    wait_q(8, 9)
+    block(own + near0[0] + near0[1], [C])
+    block(near1[0], [A, B, C])
     wait_partner(LEFT, 1)
     wait_partner(RIGHT, 0)
-    wait_ici(4)
-    wait_ici(5)
-    wait_q(12, 13, 14, 15)
+    block(near1[1], [A, B, C])
+    wait_q(10, 11, 12, 13, 14, 15)
     for r in range(1, 16):
         zz, yy = plane_back(r)
         pl.semaphore_signal(ready, inc=1, device_id=dev(zz, yy, x, c), device_id_type=MESH)
-    block(near1, [0, 1, 2])
-    block(own, [3])
-    block(near0, [3])
-    block(near1, [3])
-    block([(OPP, 0, 0), (OPP, 0, 1)], [0, 1, 2, 3])
+    block(own, [D])
+    wait_ici(4)
+    wait_ici(5)
+    block(near0[0] + near0[1] + near1[0] + near1[1], [D])
+    block(opp[0], [A, B, C, D])
     wait_partner(OPP, 0)
     wait_partner(OPP, 1)
-    block([(OPP, 1, 0), (OPP, 1, 1)], [0, 1, 2, 3])
+    block(opp[1], [A, B, C, D])
 
     b = best[...]
     hi = b.astype(BF16)
@@ -243,7 +247,7 @@
     col_sum = jnp.sum(jnp.where((lane16 >= 64) & (lane16 < 96), lse_col, 0.0), axis=0, keepdims=True)
     pos_sum = jnp.sum(jnp.sum(tops, axis=0), axis=0, keepdims=True)
     total = jnp.sum(row_sum + col_sum - jnp.where(lane1 == 96, 2.0 * pos_sum, 0.0), axis=1, keepdims=True)
-    lm_ref[...] = (total / 1024.0)[0, :1]
+    lm_ref[...] = jnp.broadcast_to(total / 1024.0, (1, 128))
 
     def to_front(v, start):
         return pltpu.roll(v, lax.rem(128 - start, 128), 1)
@@ -251,8 +255,8 @@
     pos_front = to_front(pos_q, my_slot * 4)
     my_row = jnp.sum(jnp.where(iota((8, 128), 0) == my_line, lse_row, 0.0), axis=0, keepdims=True)
     my_col = jnp.sum(jnp.where(iota((16, 128), 0) == my_slot, lse_col, 0.0), axis=0, keepdims=True)
-    lq_ref[...] = (to_front(my_row, my_slot * 4) - pos_front)[0, :4]
-    ld_ref[...] = (to_front(my_col, 64 + my_line * 4) - pos_front)[0, :4]
+    lq_ref[...] = (to_front(my_row, my_slot * 4) - pos_front)
+    ld_ref[...] = (to_front(my_col, 64 + my_line * 4) - pos_front)
     everyone.wait_send()
 
 
@@ -262,9 +266,9 @@
     def local_loss(q_hidden, d_hidden, w_proj, q_mask, d_mask, temperature):
         vmem = pl.BlockSpec(memory_space=pltpu.VMEM)
         dma = pltpu.SemaphoreType.DMA
-        return pl.pallas_call(
+        lq, ld, lm = pl.pallas_call(
             kernel,
-            out_shape=tuple(jax.ShapeDtypeStruct((n,), F32) for n in (4, 4, 1)),
+            out_shape=(jax.ShapeDtypeStruct((1, 128), F32),) * 3,
             in_specs=[vmem] * 5 + [pl.BlockSpec(memory_space=pltpu.SMEM)],
             out_specs=(vmem, vmem, vmem),
             scratch_shapes=[
@@ -279,6 +283,7 @@
             compiler_params=pltpu.CompilerParams(collective_id=0, has_side_effects=True,
                                                  vmem_limit_bytes=48 * 1024 * 1024),
         )(q_hidden, d_hidden, w_proj, q_mask, d_mask, temperature.reshape(1))
+        return lq[0, :4], ld[0, :4], lm[0, :1]
 
     return jax.shard_map(local_loss, mesh=mesh, in_specs=(batch_spec, batch_spec, P(), batch_spec, batch_spec, P()),
                          out_specs=(batch_spec, batch_spec, P('replica')), check_vma=False)

time: 35.6 us -> 34 us (0.955)
  Pallas kernels: 29.9 us -> 29.3 us
  between operations: 3.15 us -> 2.57 us
  local copies, waits for them, and re-layouts: 2.4 us -> 1.89 us
    unnamed x11 -> x9, local copies, waits for them, and re-layouts: 2.4 us -> 1.38 us
    pallas_call x1, Pallas kernels: 29.9 us -> 29.3 us  [local_loss(): pl.pallas_call(kernel, out_shape=(jax.ShapeDtypeStruct((1, 128), F32),) *...]
    squeeze x0 -> x1, local copies, waits for them, and re-layouts: none -> 0.52 us  [local_loss(): return (lq[0, :4], ld[0, :4], lm[0, :1])]
where the time goes in v4:
time: 34 us; the launch traced here: 33.8 us
  Pallas kernels  29.3 us (86%)
  between operations  2.57 us (8%)
  local copies, waits for them, and re-layouts  1.89 us (6%)
    pallas_call x1, Pallas kernels, local_loss(): pl.pallas_call(kernel, out_shape=(jax.ShapeDtypeStruct((1, 128), F32),) *...  29.3 us
    unnamed x9, local copies, waits for them, and re-layouts  1.38 us

profile of v4, /device:TPU:1, one launch (start us, length us, event | category | flops | bytes accessed | tf_op | source)
XLA Modules:
  0.0 33.8 jit_solution(2547150182693662265)
XLA Ops:
  0.6 0.0 copy-start.2
  0.6 0.0 copy-start.3
  0.7 0.0 copy-start.1
  0.7 0.0 copy-start
  1.4 1.4 %copy.9.dh = bf16[4,180,768]{2,1,0:T(8,128)(2,1)S(1)} copy(bf16[4,180,768]{2,0,1:T(4,128)(2,1)} %param.7) | data formatting | bytes 2211840 | tf_op args[1]
  2.7 0.0 copy-done.2
  2.7 0.0 copy-done.3
  2.8 0.0 copy-done.1
  2.8 0.0 copy-done
  2.8 29.3 %shard_map.85 = (f32[1,128]{1,0:T(1,128)S(1)}, f32[1,128]{1,0:T(1,128)S(1)}, f32[1,128]{1,0:T(1,128)S(1)}) custom-call(bf16[4,32,768]{2,1,0:T(8,128)(2,1)S(1)} %copy-done, bf16[4,180,768]{2,1,0:T(8,128)(2,1)S(1)} %copy.9.dh, bf16[768,128]{1,0:T(8,128)(2,1)S(1)} %copy-done.1, s32[4,32]{1,0:T(4,128)S(1)} %copy-done.3, s32[4,180]{1,0:T(4,128)S(1)} %copy-done.2, ...), custom_call_target="tpu_custom_call" | custom-call | tf_op jit(solution)/shard_map/pallas_call | solution.py:269
  32.1 0.5 %slice_bitcast_fusion = (f32[4]{0:T(128)}, f32[4]{0:T(128)}) fusion(f32[1,128]{1,0:T(1,128)S(1)} %get-tuple-element.7, f32[1,128]{1,0:T(1,128)S(1)} %get-tuple-element.6), kind=kLoop, calls=%fused_computation | loop fusion | bytes 64 | tf_op jit(solution)/shard_map/squeeze | solution.py:286
Async XLA Ops:
  0.6 2.1 %copy-start.2 = (s32[4,180]{1,0:T(4,128)S(1)}, s32[4,180]{1,0:T(4,128)}, u32[]{:S(2)}) copy-start(s32[4,180]{1,0:T(4,128)} %dm.1) | copy-start | bytes 8644
  0.6 2.1 %copy-start.3 = (s32[4,32]{1,0:T(4,128)S(1)}, s32[4,32]{1,0:T(4,128)}, u32[]{:S(2)}) copy-start(s32[4,32]{1,0:T(4,128)} %qm.1) | copy-start | bytes 1540
  0.7 2.1 %copy-start.1 = (bf16[768,128]{1,0:T(8,128)(2,1)S(1)}, bf16[768,128]{1,0:T(8,128)(2,1)}, u32[]{:S(2)}) copy-start(bf16[768,128]{1,0:T(8,128)(2,1)} %w.1) | copy-start | bytes 589828
  0.7 2.1 %copy-start = (bf16[4,32,768]{2,1,0:T(8,128)(2,1)S(1)}, bf16[4,32,768]{2,1,0:T(8,128)(2,1)}, u32[]{:S(2)}) copy-start(bf16[4,32,768]{2,1,0:T(8,128)(2,1)} %qh.1) | copy-start | bytes 589828

commit v5 on v4

--- a/solution.py
+++ b/solution.py
@@ -8,7 +8,8 @@
 F32 = jnp.float32
 BF16 = jnp.bfloat16
 MESH = pl.DeviceIdType.MESH
-DPAD = 184
+HALF = 368
+CUTS = (0, 46, 92, 136, 180)
 Q_ORDER = (0, 1, 3, 4, 12, 2, 8, 5, 7, 13, 15, 6, 14, 9, 11, 10)
 P_Y2, P_Z2, P_FAR = 5, 6, 11
 OWN, LEFT, RIGHT, OPP = 0, 1, 2, 3
@@ -22,8 +23,8 @@
     return lax.broadcasted_iota(jnp.int32, shape, axis)
 
 
-def kernel(qh, dh, w, qm, dm, temp_ref, lq_ref, ld_ref, lm_ref,
-           qbuf, dbuf, best, pick, part, qs, qr, ds_, dr, ps, pr, fs, fr, ready):
+def kernel(q_hbm, d_hbm, w_hbm, qm_hbm, dm_hbm, temp_ref, lq_ref, ld_ref, lm_ref,
+           qh, dh, w, qm, dm, lsem, live, qbuf, dbuf, best, pick, part, qs, qr, ds_, dr, ps, pr, fs, fr, ready):
     me = lax.axis_index('data')
     c = lax.rem(me, 2)
     x = lax.rem(me // 2, 4)
@@ -41,6 +42,14 @@
 
     def line_back(r):
         return lax.rem(x + 4 - r // 2, 4), lax.rem(c + r % 2, 2)
+
+    loads = [pltpu.make_async_copy(dm_hbm, dm, lsem.at[0]), pltpu.make_async_copy(w_hbm, w, lsem.at[1])]
+    for i in range(4):
+        rows = pl.ds(CUTS[i], CUTS[i + 1] - CUTS[i])
+        loads.append(pltpu.make_async_copy(d_hbm.at[rows], dh.at[rows], lsem.at[2 + i]))
+    loads += [pltpu.make_async_copy(q_hbm, qh, lsem.at[6]), pltpu.make_async_copy(qm_hbm, qm, lsem.at[7])]
+    for cp in loads:
+        cp.start()
 
     barrier = pltpu.get_barrier_semaphore()
     for r in Q_ORDER[1:P_FAR]:
@@ -50,23 +59,29 @@
         xx, cc = line_back(r)
         pl.semaphore_signal(barrier, inc=1, device_id=dev(z, y, xx, cc), device_id_type=MESH)
 
+    loads[0].wait()
+    d_col = jnp.transpose(jnp.concatenate([dm[...].astype(F32), jnp.zeros((4, 180), F32)], axis=0))
+    for j in range(4):
+        live[pl.ds(j, 180, stride=4), :] = jnp.broadcast_to(d_col[:, j:j + 1], (180, 128))
+    valid = live[...].reshape(90, 8, 128) == 1.0
+    token = (iota((720, 128), 0) // 4).reshape(90, 8, 128)
+    first = jnp.min(jnp.where(valid, token, 1000), axis=0)
+    first = jnp.minimum(first, pltpu.roll(first, 4, 0))
+    for cp in loads[1:]:
+        cp.wait()
+
+    halves = [dh[0:92].reshape(HALF, 768), dh[92:180].reshape(720 - HALF, 768)]
+    u = jnp.concatenate([unit_rows(jnp.dot(rows, w[...], preferred_element_type=F32)) for rows in halves], axis=0)
+    u = u.reshape(90, 8, 128)
+    vec = jnp.sum(jnp.where(token == first[None], u, 0.0), axis=0)
+    vec = vec + pltpu.roll(vec, 4, 0)
+    dbuf[OWN, 0] = jnp.where(valid, u, vec[None]).reshape(720, 128).astype(BF16)
+
     q_raw = jnp.dot(qh[...].reshape(128, 768), w[...], preferred_element_type=F32)
     q_col = jnp.transpose(jnp.concatenate([qm[...].astype(F32), jnp.zeros((4, 32), F32)], axis=0))
     q_valid = jnp.concatenate([q_col[:, i:i + 1] for i in range(4)], axis=0)
     qbuf[0] = jnp.where(q_valid == 1.0, unit_rows(q_raw), 0.0).astype(BF16)
 
-    d_col = jnp.transpose(jnp.concatenate([dm[...].astype(F32), jnp.zeros((4, 180), F32)], axis=0))
-    pos = iota((180, 1), 0)
-    for h in range(2):
-        parts = []
-        for j in (2 * h, 2 * h + 1):
-            u = unit_rows(jnp.dot(dh[j], w[...], preferred_element_type=F32))
-            valid = d_col[:, j:j + 1] == 1.0
-            first = jnp.min(jnp.where(valid, pos, 1000), axis=0, keepdims=True)
-            vec = jnp.sum(jnp.where(pos == first, u, 0.0), axis=0, keepdims=True)
-            parts += [jnp.where(valid, u, vec), jnp.broadcast_to(vec, (DPAD - 180, 128))]
-        dbuf[OWN, 0, h] = jnp.concatenate(parts, axis=0).astype(BF16)
-
     pl.semaphore_wait(barrier, 17)
 
     xr, xl = lax.rem(x + 1, 4), lax.rem(x + 3, 4)
@@ -82,14 +97,16 @@
 
     ICI = [(LEFT, 0), (RIGHT, 1), (LEFT, 1), (RIGHT, 0), (OPP, 0), (OPP, 1)]
 
+    SPAN = (pl.ds(0, HALF), pl.ds(HALF, 720 - HALF))
+
     def to_right(src, h, i):
-        return rdma(dbuf.at[src, 0, h], dbuf.at[ICI[i][0], 0, h], ds_.at[i], dr.at[i], right)
+        return rdma(dbuf.at[src, 0, SPAN[h]], dbuf.at[ICI[i][0], 0, SPAN[h]], ds_.at[i], dr.at[i], right)
 
     def to_left(src, h, i):
-        return rdma(dbuf.at[src, 0, h], dbuf.at[ICI[i][0], 0, h], ds_.at[i], dr.at[i], left)
+        return rdma(dbuf.at[src, 0, SPAN[h]], dbuf.at[ICI[i][0], 0, SPAN[h]], ds_.at[i], dr.at[i], left)
 
     def to_partner(src, h):
-        return rdma(dbuf.at[src, 0, h], dbuf.at[src, 1, h], ps.at[2 * src + h], pr.at[2 * src + h], partner)
+        return rdma(dbuf.at[src, 0, SPAN[h]], dbuf.at[src, 1, SPAN[h]], ps.at[2 * src + h], pr.at[2 * src + h], partner)
 
     def q_copy(p):
         dz, dy = Q_ORDER[p] // 4, Q_ORDER[p] % 4
@@ -139,16 +156,17 @@
             q_copy(p).wait_recv()
 
     def block(pieces, chunks):
-        n = len(pieces)
-        lhs = jnp.concatenate([dbuf[piece] for piece in pieces], axis=0)
+        lhs = jnp.concatenate([dbuf[side, core, SPAN[h], :] for side, core, h in pieces], axis=0)
         for lo, hi in chunks:
             width = (hi - lo) * 128
             rhs = qbuf[lo:hi].reshape(width, 128)
             sim = lax.dot_general(lhs, rhs, (((1,), (1,)), ((), ())), preferred_element_type=F32)
-            top = jnp.max(sim.reshape(2 * n, DPAD, width), axis=1)
-            for i, (side, core, h) in enumerate(pieces):
-                row = side * 8 + core * 4 + h * 2
-                best[row:row + 2, lo * 128:hi * 128] = top[2 * i:2 * i + 2]
+            at = 0
+            for side, core, h in pieces:
+                rows = HALF if h == 0 else 720 - HALF
+                top = jnp.max(sim[at:at + rows].reshape(rows // 8, 8, width), axis=0)
+                best[side, core, h, :, lo * 128:hi * 128] = top
+                at += rows
 
     def pair(core, *halves):
         return [(side, core, h) for side, h in halves]
@@ -196,7 +214,12 @@
     wait_partner(OPP, 1)
     block(opp[1], [A, B, C, D])
 
-    b = best[...]
+    def fold(side, core):
+        a = jnp.maximum(best[side, core, 0], best[side, core, 1])
+        return jnp.maximum(a, pltpu.roll(a, 4, 0))
+
+    upper = iota((8, 2048), 0) < 4
+    b = jnp.concatenate([jnp.where(upper, fold(side, 0), fold(side, 1)) for side in range(4)], axis=0)
     hi = b.astype(BF16)
     rest = b - hi.astype(F32)
     mid = rest.astype(BF16)
@@ -265,16 +288,24 @@
 
     def local_loss(q_hidden, d_hidden, w_proj, q_mask, d_mask, temperature):
         vmem = pl.BlockSpec(memory_space=pltpu.VMEM)
+        hbm = pl.BlockSpec(memory_space=pltpu.HBM)
         dma = pltpu.SemaphoreType.DMA
         lq, ld, lm = pl.pallas_call(
             kernel,
             out_shape=(jax.ShapeDtypeStruct((1, 128), F32),) * 3,
-            in_specs=[vmem] * 5 + [pl.BlockSpec(memory_space=pltpu.SMEM)],
+            in_specs=[hbm] * 5 + [pl.BlockSpec(memory_space=pltpu.SMEM)],
             out_specs=(vmem, vmem, vmem),
             scratch_shapes=[
+                pltpu.VMEM((4, 32, 768), BF16),
+                pltpu.VMEM((180, 4, 768), BF16),
+                pltpu.VMEM((768, 128), BF16),
+                pltpu.VMEM((4, 32), jnp.int32),
+                pltpu.VMEM((4, 180), jnp.int32),
+                dma((8,)),
+                pltpu.VMEM((720, 128), F32),
                 pltpu.VMEM((16, 128, 128), BF16),
-                pltpu.VMEM((4, 2, 2, 2 * DPAD, 128), BF16),
-                pltpu.VMEM((32, 2048), F32),
+                pltpu.VMEM((4, 2, 720, 128), BF16),
+                pltpu.VMEM((4, 2, 2, 8, 2048), F32),
                 pltpu.VMEM((2048, 128), BF16),
                 pltpu.VMEM((128, 2, 128), F32),
                 dma((16,)), dma((16,)), dma((6,)), dma((6,)), dma((8,)), dma((8,)), dma, dma,
@@ -282,7 +313,8 @@
             ],
             compiler_params=pltpu.CompilerParams(collective_id=0, has_side_effects=True,
                                                  vmem_limit_bytes=48 * 1024 * 1024),
-        )(q_hidden, d_hidden, w_proj, q_mask, d_mask, temperature.reshape(1))
+        )(*[pltpu.with_memory_space_constraint(a, pltpu.HBM)
+            for a in (q_hidden, jnp.swapaxes(d_hidden, 0, 1), w_proj, q_mask, d_mask)], temperature.reshape(1))
         return lq[0, :4], ld[0, :4], lm[0, :1]
 
     return jax.shard_map(local_loss, mesh=mesh, in_specs=(batch_spec, batch_spec, P(), batch_spec, batch_spec, P()),

time: 34 us -> 32.4 us (0.953)
  local copies, waits for them, and re-layouts: 1.89 us -> 0.52 us
    unnamed x9 -> x0, local copies, waits for them, and re-layouts: 1.38 us -> none
where the time goes in v5:
time: 32.4 us; the launch traced here: 32.2 us
  Pallas kernels  29.3 us (90%)
  between operations  2.45 us (8%)
  local copies, waits for them, and re-layouts  0.52 us (2%)
    pallas_call x1, Pallas kernels, local_loss(): pl.pallas_call(kernel, out_shape=(jax.ShapeDtypeStruct((1, 128), F32),) *...  29.3 us

profile of v5, /device:TPU:1, one launch (start us, length us, event | category | flops | bytes accessed | tf_op | source)
XLA Modules:
  0.0 32.2 jit_solution(17984855467842070717)
XLA Ops:
  1.3 29.3 %shard_map.85 = (f32[1,128]{1,0:T(1,128)S(1)}, f32[1,128]{1,0:T(1,128)S(1)}, f32[1,128]{1,0:T(1,128)S(1)}) custom-call(bf16[4,32,768]{2,1,0:T(8,128)(2,1)} %q_hbm.1, bf16[180,4,768]{2,1,0:T(4,128)(2,1)} %bitcast.10, bf16[768,128]{1,0:T(8,128)(2,1)} %w_hbm.1, s32[4,32]{1,0:T(4,128)} %qm_hbm.1, s32[4,180]{1,0:T(4,128)} %dm_hbm.1, f32[1]{0:T(128)} %bitcast.8.temp_ref), custom_call_target="tpu_custom_call" | custom-call | tf_op jit(solution)/shard_map/pallas_call | solution.py:293
  30.5 0.5 %slice_bitcast_fusion = (f32[4]{0:T(128)}, f32[4]{0:T(128)}) fusion(f32[1,128]{1,0:T(1,128)S(1)} %get-tuple-element.7, f32[1,128]{1,0:T(1,128)S(1)} %get-tuple-element.6), kind=kLoop, calls=%fused_computation | loop fusion | bytes 64 | tf_op jit(solution)/shard_map/squeeze | solution.py:318

commit v6 on v5

--- a/solution.py
+++ b/solution.py
@@ -179,11 +179,11 @@
 
     wait_partner(OWN, 0)
     wait_partner(OWN, 1)
-    wait_q(1, 2, 3)
-    block(own, [A])
     wait_q(P_Y2, P_Z2)
     for p in range(P_FAR, 16):
         send(q_copy(p))
+    wait_q(1, 2, 3)
+    block(own, [A])
     wait_ici(0)
     wait_ici(1)
     block(near0[0], [A])
@@ -205,10 +205,9 @@
     for r in range(1, 16):
         zz, yy = plane_back(r)
         pl.semaphore_signal(ready, inc=1, device_id=dev(zz, yy, x, c), device_id_type=MESH)
-    block(own, [D])
     wait_ici(4)
     wait_ici(5)
-    block(near0[0] + near0[1] + near1[0] + near1[1], [D])
+    block(own + near0[0] + near0[1] + near1[0] + near1[1], [D])
     block(opp[0], [A, B, C, D])
     wait_partner(OPP, 0)
     wait_partner(OPP, 1)

time: 32.4 us -> 32.2 us (level)
  no operation moved by 1% of the time
where the time goes in v6:
time: 32.2 us; the launch traced here: 32 us
  Pallas kernels  29.1 us (90%)
  between operations  2.45 us (8%)
  local copies, waits for them, and re-layouts  0.52 us (2%)
    pallas_call x1, Pallas kernels, local_loss(): pl.pallas_call(kernel, out_shape=(jax.ShapeDtypeStruct((1, 128), F32),) *...  29.1 us

profile of v6, /device:TPU:1, one launch (start us, length us, event | category | flops | bytes accessed | tf_op | source)
XLA Modules:
  0.0 32.0 jit_solution(12321619558303494155)
XLA Ops:
  1.3 29.1 %shard_map.85 = (f32[1,128]{1,0:T(1,128)S(1)}, f32[1,128]{1,0:T(1,128)S(1)}, f32[1,128]{1,0:T(1,128)S(1)}) custom-call(bf16[4,32,768]{2,1,0:T(8,128)(2,1)} %q_hbm.1, bf16[180,4,768]{2,1,0:T(4,128)(2,1)} %bitcast.10, bf16[768,128]{1,0:T(8,128)(2,1)} %w_hbm.1, s32[4,32]{1,0:T(4,128)} %qm_hbm.1, s32[4,180]{1,0:T(4,128)} %dm_hbm.1, f32[1]{0:T(128)} %bitcast.8.temp_ref), custom_call_target="tpu_custom_call" | custom-call | tf_op jit(solution)/shard_map/pallas_call | solution.py:292
  30.4 0.5 %slice_bitcast_fusion = (f32[4]{0:T(128)}, f32[4]{0:T(128)}) fusion(f32[1,128]{1,0:T(1,128)S(1)} %get-tuple-element.7, f32[1,128]{1,0:T(1,128)S(1)} %get-tuple-element.6), kind=kLoop, calls=%fused_computation | loop fusion | bytes 64 | tf_op jit(solution)/shard_map/squeeze | solution.py:317

commit v7 on v6

--- a/solution.py
+++ b/solution.py
@@ -95,7 +95,7 @@
         cp.start()
         sends.append(cp)
 
-    ICI = [(LEFT, 0), (RIGHT, 1), (LEFT, 1), (RIGHT, 0), (OPP, 0), (OPP, 1)]
+    ICI = [(LEFT, 1), (RIGHT, 0)]
 
     SPAN = (pl.ds(0, HALF), pl.ds(HALF, 720 - HALF))
 
@@ -104,6 +104,14 @@
 
     def to_left(src, h, i):
         return rdma(dbuf.at[src, 0, SPAN[h]], dbuf.at[ICI[i][0], 0, SPAN[h]], ds_.at[i], dr.at[i], left)
+
+    PARTS = ((pl.ds(0, 192), pl.ds(192, 176)), (pl.ds(HALF, 176), pl.ds(HALF + 176, 176)))
+
+    def along(src, h, part):
+        dst = OPP if src != OWN else (LEFT, RIGHT)[h]
+        k = h + 2 * part + (6 if src != OWN else 2)
+        rows = PARTS[h][part]
+        return rdma(dbuf.at[src, 0, rows], dbuf.at[dst, 0, rows], ds_.at[k], dr.at[k], (right, left)[h])
 
     def to_partner(src, h):
         return rdma(dbuf.at[src, 0, SPAN[h]], dbuf.at[src, 1, SPAN[h]], ps.at[2 * src + h], pr.at[2 * src + h], partner)
@@ -119,14 +127,15 @@
         zz, yy = plane_back(4 * dz + dy)
         return rdma(qbuf.at[src], qbuf.at[p], qs.at[p], qr.at[p], dev(zz, yy, x, c))
 
-    send(to_right(OWN, 0, 0))
-    send(to_left(OWN, 1, 1))
+    for part_ in range(2):
+        send(along(OWN, 0, part_))
+        send(along(OWN, 1, part_))
     for p in (P_Y2, P_Z2, 1, 2, 3, 4):
         send(q_copy(p))
     send(to_partner(OWN, 0))
     send(to_partner(OWN, 1))
-    send(to_right(OWN, 1, 2))
-    send(to_left(OWN, 0, 3))
+    send(to_right(OWN, 1, 0))
+    send(to_left(OWN, 0, 1))
     for p in range(P_Z2 + 1, P_FAR):
         send(q_copy(p))
 
@@ -139,14 +148,23 @@
     for p in range(16):
         pick[p * 128:(p + 1) * 128, :] = (tok + 4 * plane_slot(Q_ORDER[p]) == lanes).astype(F32).astype(BF16)
 
-    def wait_ici(i):
-        side, h = ICI[i]
-        to_right(OWN, h, i).wait_recv()
-        if i == 0:
-            send(to_right(LEFT, 0, 4))
-        if i == 1:
-            send(to_left(RIGHT, 1, 5))
-        send(to_partner(side, h))
+    def wait_first(part_):
+        for h in range(2):
+            along(OWN, h, part_).wait_recv()
+            send(along((LEFT, RIGHT)[h], h, part_))
+            if part_ == 1:
+                send(to_partner((LEFT, RIGHT)[h], h))
+
+    def wait_second():
+        for i, (side, h) in enumerate(ICI):
+            to_right(OWN, h, i).wait_recv()
+            send(to_partner(side, h))
+
+    def wait_opp():
+        for h in range(2):
+            for part_ in range(2):
+                along((LEFT, RIGHT)[h], h, part_).wait_recv()
+            send(to_partner(OPP, h))
 
     def wait_partner(side, h):
         to_partner(side, h).wait_recv()
@@ -179,13 +197,13 @@
 
     wait_partner(OWN, 0)
     wait_partner(OWN, 1)
+    wait_first(0)
     wait_q(P_Y2, P_Z2)
     for p in range(P_FAR, 16):
         send(q_copy(p))
     wait_q(1, 2, 3)
     block(own, [A])
-    wait_ici(0)
-    wait_ici(1)
+    wait_first(1)
     block(near0[0], [A])
     wait_q(4, 7)
     block(own, [B])
@@ -193,8 +211,7 @@
     wait_partner(LEFT, 0)
     wait_partner(RIGHT, 1)
     block(near0[1], [A, B])
-    wait_ici(2)
-    wait_ici(3)
+    wait_second()
     wait_q(8, 9)
     block(own + near0[0] + near0[1], [C])
     block(near1[0], [A, B, C])
@@ -205,8 +222,7 @@
     for r in range(1, 16):
         zz, yy = plane_back(r)
         pl.semaphore_signal(ready, inc=1, device_id=dev(zz, yy, x, c), device_id_type=MESH)
-    wait_ici(4)
-    wait_ici(5)
+    wait_opp()
     block(own + near0[0] + near0[1] + near1[0] + near1[1], [D])
     block(opp[0], [A, B, C, D])
     wait_partner(OPP, 0)
@@ -307,7 +323,7 @@
                 pltpu.VMEM((4, 2, 2, 8, 2048), F32),
                 pltpu.VMEM((2048, 128), BF16),
                 pltpu.VMEM((128, 2, 128), F32),
-                dma((16,)), dma((16,)), dma((6,)), dma((6,)), dma((8,)), dma((8,)), dma, dma,
+                dma((16,)), dma((16,)), dma((10,)), dma((10,)), dma((8,)), dma((8,)), dma, dma,
                 pltpu.SemaphoreType.REGULAR,
             ],
             compiler_params=pltpu.CompilerParams(collective_id=0, has_side_effects=True,

time: 32.2 us -> 32 us (level)
  no operation moved by 1% of the time
where the time goes in v7:
time: 32 us; the launch traced here: 31.9 us
  Pallas kernels  28.9 us (90%)
  between operations  2.45 us (8%)
  local copies, waits for them, and re-layouts  0.52 us (2%)
    pallas_call x1, Pallas kernels, local_loss(): pl.pallas_call(kernel, out_shape=(jax.ShapeDtypeStruct((1, 128), F32),) *...  28.9 us

profile of v7, /device:TPU:1, one launch (start us, length us, event | category | flops | bytes accessed | tf_op | source)
XLA Modules:
  0.0 31.9 jit_solution(16654893091396549159)
XLA Ops:
  1.3 28.9 %shard_map.85 = (f32[1,128]{1,0:T(1,128)S(1)}, f32[1,128]{1,0:T(1,128)S(1)}, f32[1,128]{1,0:T(1,128)S(1)}) custom-call(bf16[4,32,768]{2,1,0:T(8,128)(2,1)} %q_hbm.1, bf16[180,4,768]{2,1,0:T(4,128)(2,1)} %bitcast.10, bf16[768,128]{1,0:T(8,128)(2,1)} %w_hbm.1, s32[4,32]{1,0:T(4,128)} %qm_hbm.1, s32[4,180]{1,0:T(4,128)} %dm_hbm.1, f32[1]{0:T(128)} %bitcast.8.temp_ref), custom_call_target="tpu_custom_call" | custom-call | tf_op jit(solution)/shard_map/pallas_call | solution.py:308
  30.2 0.5 %slice_bitcast_fusion = (f32[4]{0:T(128)}, f32[4]{0:T(128)}) fusion(f32[1,128]{1,0:T(1,128)S(1)} %get-tuple-element.7, f32[1,128]{1,0:T(1,128)S(1)} %get-tuple-element.6), kind=kLoop, calls=%fused_computation | loop fusion | bytes 64 | tf_op jit(solution)/shard_map/squeeze | solution.py:333

commit v8 on v7

--- a/solution.py
+++ b/solution.py
@@ -63,7 +63,7 @@
     d_col = jnp.transpose(jnp.concatenate([dm[...].astype(F32), jnp.zeros((4, 180), F32)], axis=0))
     for j in range(4):
         live[pl.ds(j, 180, stride=4), :] = jnp.broadcast_to(d_col[:, j:j + 1], (180, 128))
-    valid = live[...].reshape(90, 8, 128) == 1.0
+    valid = live[0:720].reshape(90, 8, 128) == 1.0
     token = (iota((720, 128), 0) // 4).reshape(90, 8, 128)
     first = jnp.min(jnp.where(valid, token, 1000), axis=0)
     first = jnp.minimum(first, pltpu.roll(first, 4, 0))
@@ -317,7 +317,7 @@
                 pltpu.VMEM((4, 32), jnp.int32),
                 pltpu.VMEM((4, 180), jnp.int32),
                 dma((8,)),
-                pltpu.VMEM((720, 128), F32),
+                pltpu.VMEM((736, 128), F32),
                 pltpu.VMEM((16, 128, 128), BF16),
                 pltpu.VMEM((4, 2, 720, 128), BF16),
                 pltpu.VMEM((4, 2, 2, 8, 2048), F32),

time: 32 us -> 32 us (level)
  no operation moved by 1% of the time
where the time goes in v8:
time: 32 us; the launch traced here: 31.9 us
  Pallas kernels  28.9 us (90%)
  between operations  2.45 us (8%)
  local copies, waits for them, and re-layouts  0.52 us (2%)
    pallas_call x1, Pallas kernels, local_loss(): pl.pallas_call(kernel, out_shape=(jax.ShapeDtypeStruct((1, 128), F32),) *...  28.9 us

profile of v8, /device:TPU:1, one launch (start us, length us, event | category | flops | bytes accessed | tf_op | source)
XLA Modules:
  0.0 31.9 jit_solution(12318556481166145980)
XLA Ops:
  1.3 28.9 %shard_map.85 = (f32[1,128]{1,0:T(1,128)S(1)}, f32[1,128]{1,0:T(1,128)S(1)}, f32[1,128]{1,0:T(1,128)S(1)}) custom-call(bf16[4,32,768]{2,1,0:T(8,128)(2,1)} %q_hbm.1, bf16[180,4,768]{2,1,0:T(4,128)(2,1)} %bitcast.10, bf16[768,128]{1,0:T(8,128)(2,1)} %w_hbm.1, s32[4,32]{1,0:T(4,128)} %qm_hbm.1, s32[4,180]{1,0:T(4,128)} %dm_hbm.1, f32[1]{0:T(128)} %bitcast.8.temp_ref), custom_call_target="tpu_custom_call" | custom-call | tf_op jit(solution)/shard_map/pallas_call | solution.py:308
  30.2 0.5 %slice_bitcast_fusion = (f32[4]{0:T(128)}, f32[4]{0:T(128)}) fusion(f32[1,128]{1,0:T(1,128)S(1)} %get-tuple-element.7, f32[1,128]{1,0:T(1,128)S(1)} %get-tuple-element.6), kind=kLoop, calls=%fused_computation | loop fusion | bytes 64 | tf_op jit(solution)/shard_map/squeeze | solution.py:333
